TPU v7x, 128 devices: a whole 4x4x4 slice. The times are simulated.
128 devices in a mesh: dp: 1, row: 2 (over core), col: 64 (over z, y, x).
Axes of the slice: x: 4, y: 4, z: 4, core: 2. Of those that a mesh axis runs over, the one named last changes fastest.
Arguments:
- x: bfloat16 [2, 128, 128, 2048], P(None, ('dp', 'row', 'col'))
- idx: int32 [2, 128, 128, 8], P(None, ('dp', 'row', 'col'))
- gates: float32 [2, 128, 128, 8], P(None, ('dp', 'row', 'col'))
- wq: bfloat16 [2048, 4096], replicated
- wk: bfloat16 [2048, 4096], replicated
- wv: bfloat16 [2048, 4096], replicated
- wo: bfloat16 [4096, 2048], replicated
- gattn: float32 [2048], replicated
- gmoe: float32 [2048], replicated
- w1: bfloat16 [128, 2048, 768], P(('row', 'col'))
- w3: bfloat16 [128, 2048, 768], P(('row', 'col'))
- w2: bfloat16 [128, 768, 2048], P(('row', 'col'))
Outputs:
- output: bfloat16 [2, 128, 128, 2048], P(None, ('dp', 'row', 'col'))
All inputs are finite; a program needn't handle non-finite values.
Results may differ from a plain program's by a relative error of at most 0.0107599.
Values are sent between devices in bfloat16 or wider.
A program may use at most 1 GiB of HBM per device.

v0:
```python
import jax
import jax.numpy as jnp
from jax import lax
from jax.sharding import PartitionSpec as P

HEAD = 128


def rms(v, g):
    vf = v.astype(jnp.float32)
    return (vf * lax.rsqrt(jnp.mean(vf * vf, axis=-1, keepdims=True) + 1e-6) * g).astype(jnp.bfloat16)


def attention(x, wq, wk, wv, wo, g):
    ns, seq, d = x.shape
    nh = wq.shape[1] // HEAD
    xf = x.reshape(ns * seq, d)
    u = rms(xf, g)

    def proj(w):
        a = jnp.dot(u, w, preferred_element_type=jnp.float32).astype(jnp.bfloat16)
        return a.reshape(ns, seq, nh, HEAD)

    q, k, v = proj(wq), proj(wk), proj(wv)
    causal = jnp.arange(seq)[:, None] >= jnp.arange(seq)[None, :]
    s = jnp.einsum("bqhe,bkhe->bhqk", q, k, preferred_element_type=jnp.float32) * HEAD ** -0.5
    s = jnp.where(causal, s, -1e30)
    p = jax.nn.softmax(s, axis=-1).astype(jnp.bfloat16)
    o = jnp.einsum("bhqk,bkhe->bqhe", p, v, preferred_element_type=jnp.float32).astype(jnp.bfloat16)
    o = o.reshape(ns * seq, nh * HEAD)
    a = jnp.dot(o, wo, preferred_element_type=jnp.float32)
    return (xf.astype(jnp.float32) + a).astype(jnp.bfloat16)


def capacity(t, top, n_exp):
    return ((top * ((2 * t + n_exp - 1) // n_exp) + 7) // 8) * 8


def slots(idx, n_exp, cap):
    t = idx.shape[0]
    hit = idx[:, :, None] == jnp.arange(n_exp, dtype=idx.dtype)
    cnt = jnp.sum(hit, axis=1).astype(jnp.bfloat16)
    tri = (jnp.arange(t)[:, None] > jnp.arange(t)[None, :]).astype(jnp.bfloat16)
    before = jnp.dot(tri, cnt, preferred_element_type=jnp.float32)
    pos = jnp.sum(jnp.where(hit, before[:, None, :], 0.0), axis=-1).astype(jnp.int32)
    return idx * cap + pos


def route(row, n):
    return row[:, :, None] == jnp.arange(n, dtype=row.dtype)


def dispatch(hit, z):
    sel = jnp.any(hit, axis=1).astype(jnp.bfloat16)
    return jnp.einsum("tr,td->rd", sel, z, preferred_element_type=jnp.float32).astype(jnp.bfloat16)


def combine(hit, g, back):
    t = g.shape[0]
    parts = []
    rest = g
    for _ in range(3):
        piece = rest.astype(jnp.bfloat16)
        parts.append(piece)
        rest = rest - piece.astype(jnp.float32)
    pieces = jnp.stack(parts)
    w = jnp.sum(jnp.where(hit[None], pieces[..., None], jnp.zeros((), jnp.bfloat16)), axis=2)
    out = jnp.dot(w.reshape(3 * t, -1), back, preferred_element_type=jnp.float32).reshape(3, t, -1)
    return out[0] + out[1] + out[2]


def solution(mesh):
    ep_axes = ("row", "col")
    tok_axes = ("dp", "row", "col")
    ep = mesh.shape["row"] * mesh.shape["col"]

    def local(x, idx, gates, wq, wk, wv, wo, gattn, gmoe, w1, w3, w2):
        ns, seq, d = x.shape[1:]
        t = ns * seq
        top = idx.shape[-1]
        el = w1.shape[0]
        n_exp = el * ep
        cap = capacity(t, top, n_exp)
        ys = []
        for m in range(2):
            h = attention(x[m], wq, wk, wv, wo, gattn)
            z = rms(h, gmoe)
            slot = slots(idx[m].reshape(t, top), n_exp, cap)
            hit = route(slot, n_exp * cap)
            buf = dispatch(hit, z)
            recv = lax.all_to_all(buf.reshape(ep, el * cap, d), ep_axes, 0, 0, tiled=True)
            recv = recv.reshape(ep, el, cap, d)
            h1 = jnp.einsum("secd,edf->secf", recv, w1, preferred_element_type=jnp.float32)
            h3 = jnp.einsum("secd,edf->secf", recv, w3, preferred_element_type=jnp.float32)
            act = (jax.nn.silu(h1) * h3).astype(jnp.bfloat16)
            out = jnp.einsum("secf,efd->secd", act, w2, preferred_element_type=jnp.float32).astype(jnp.bfloat16)
            back = lax.all_to_all(out.reshape(ep, el * cap, d), ep_axes, 0, 0, tiled=True)
            back = back.reshape(n_exp * cap, d)
            acc = combine(hit, gates[m].reshape(t, top), back)
            y = (h.astype(jnp.float32) + acc).astype(jnp.bfloat16)
            ys.append(y.reshape(ns, seq, d))
        return jnp.stack(ys)

    tok_spec = P(None, tok_axes)
    exp_spec = P(ep_axes)
    return jax.shard_map(local, mesh=mesh,
                         in_specs=(tok_spec, tok_spec, tok_spec, P(), P(), P(), P(), P(), P(), exp_spec, exp_spec, exp_spec),
                         out_specs=tok_spec, check_vma=False)
```

profile of v0, /device:TPU:3, one launch (start us, length us, event | category | flops | bytes accessed | tf_op | source)
XLA Modules:
  0.0 618.4 jit_solution(10281722755093879623)
XLA Ops:
  1.7 9.4 %convolution_convert_fusion.6 = bf16[128,4096]{1,0:T(8,128)(2,1)} fusion(bf16[2048,4096]{1,0:T(8,128)(2,1)} %param.17, f32[128]{0:T(128)S(1)} %get-tuple-element.26, f32[2048]{0:T(1024)} %param.19, bf16[2,1,128,2048]{3,2,1,0:T(8,128)(2,1)} %param.12), kind=kOutput, calls=%fused_computation.34 | convolution fusion | flops 2149056512 | bytes 18358784 | tf_op jit(solution)/shard_map/dot_general | solution.py:21
  13.4 8.5 %fusion.53 = bf16[16,32,8,128]{3,2,1,0:T(8,128)(2,1)S(1)} fusion(bf16[2048,4096]{1,0:T(8,128)(2,1)} %param.16, f32[128]{0:T(128)S(1)} %get-tuple-element.26, f32[2048]{0:T(1024)S(1)} %copy-done.9, bf16[2,1,128,2048]{3,2,1,0:T(8,128)(2,1)} %param.12), kind=kOutput, calls=%fused_computation.69 | convolution fusion | flops 2149056512 | bytes 18358784 | tf_op jit(solution)/shard_map/dot_general | solution.py:21
  21.9 8.6 %fusion.52 = bf16[16,32,8,128]{3,2,1,0:T(8,128)(2,1)S(1)} fusion(bf16[2048,4096]{1,0:T(8,128)(2,1)} %param.15, f32[128]{0:T(128)S(1)} %get-tuple-element.26, f32[2048]{0:T(1024)S(1)} %copy-done.9, bf16[2,1,128,2048]{3,2,1,0:T(8,128)(2,1)S(1)} %copy-done.1), kind=kOutput, calls=%fused_computation.68 | convolution fusion | flops 2149056512 | bytes 18358784 | tf_op jit(solution)/shard_map/dot_general | solution.py:21
  37.2 5.1 fusion.89
  45.9 8.6 %multiply_reduce_fusion = (f32[128]{0:T(128)S(1)}, f32[128,2048]{1,0:T(8,128)S(1)}) fusion(bf16[128,4096]{0,1:T(8,128)(2,1)} %bitcast.219, bf16[4096,2048]{1,0:T(8,128)(2,1)} %param.18, bf16[2,1,128,2048]{3,2,1,0:T(8,128)(2,1)} %param.12), kind=kOutput, calls=%fused_computation.96 | convolution fusion | flops 2149056512 | bytes 19399168 | tf_op jit(solution)/shard_map/dot_general | solution.py:31
  54.5 5.6 convolution_convert_fusion
  60.2 11.3 %all-to-all-start.2 = ((bf16[128,16,2048]{2,1,0:T(8,128)(2,1)}), bf16[128,16,2048]{2,1,0:T(8,128)(2,1)}, u32[]{:S(2)}, u32[]{:S(2)}) async-start(bf16[128,16,2048]{2,1,0:T(8,128)(2,1)} %bitcast.216), calls=%async_computation.2 | async-start | bytes 16777216 | tf_op jit(solution)/shard_map/all_to_all | solution.py:91
  71.4 9.4 %convolution_convert_fusion.9 = bf16[128,4096]{1,0:T(8,128)(2,1)} fusion(bf16[2048,4096]{1,0:T(8,128)(2,1)} %param.17, f32[2048]{0:T(1024)S(1)} %copy-done.9, f32[128]{0:T(128)S(1)} %get-tuple-element.27, bf16[2,1,128,2048]{3,2,1,0:T(8,128)(2,1)} %param.12), kind=kOutput, calls=%fused_computation.37 | convolution fusion | flops 2149056512 | bytes 18358784 | tf_op jit(solution)/shard_map/dot_general | solution.py:21
  84.4 9.5 %fusion.51 = bf16[16,32,8,128]{3,2,1,0:T(8,128)(2,1)} fusion(bf16[2048,4096]{1,0:T(8,128)(2,1)} %param.16, f32[2048]{0:T(1024)S(1)} %copy-done.9, f32[128]{0:T(128)S(1)} %get-tuple-element.27, bf16[2,1,128,2048]{3,2,1,0:T(8,128)(2,1)} %param.12), kind=kOutput, calls=%fused_computation.67 | convolution fusion | flops 2149056512 | bytes 18358784 | tf_op jit(solution)/shard_map/dot_general | solution.py:21
  93.9 9.2 %fusion.50 = bf16[16,32,8,128]{3,2,1,0:T(8,128)(2,1)} fusion(bf16[2048,4096]{1,0:T(8,128)(2,1)} %param.15, f32[2048]{0:T(1024)S(1)} %copy-done.9, f32[128]{0:T(128)S(1)} %get-tuple-element.27, bf16[2,1,128,2048]{3,2,1,0:T(8,128)(2,1)S(1)} %copy-done.2), kind=kOutput, calls=%fused_computation.66 | convolution fusion | flops 2149056512 | bytes 18358784 | tf_op jit(solution)/shard_map/dot_general | solution.py:21
  105.7 3.7 fusion.65
  109.4 3.7 convolution_convert_fusion.11
  113.1 8.5 %multiply_reduce_fusion.1 = (f32[128]{0:T(128)S(1)}, f32[128,2048]{1,0:T(8,128)S(1)}) fusion(bf16[128,4096]{0,1:T(8,128)(2,1)} %bitcast.218, bf16[4096,2048]{1,0:T(8,128)(2,1)} %param.18, bf16[2,1,128,2048]{3,2,1,0:T(8,128)(2,1)} %param.12), kind=kOutput, calls=%fused_computation.99 | convolution fusion | flops 2149056512 | bytes 19399168 | tf_op jit(solution)/shard_map/dot_general | solution.py:31
  121.7 5.0 fusion.88
  126.7 5.6 convolution_convert_fusion.1
  132.3 60.3 %all-to-all-done.2 = bf16[128,16,2048]{2,1,0:T(8,128)(2,1)} async-done(((bf16[128,16,2048]{2,1,0:T(8,128)(2,1)}), bf16[128,16,2048]{2,1,0:T(8,128)(2,1)}, u32[]{:S(2)}, u32[]{:S(2)}) %all-to-all-start.2) | async-done | bytes 8388640 | tf_op jit(solution)/shard_map/all_to_all | solution.py:91
  192.6 21.7 %all-to-all-start = ((bf16[128,16,2048]{2,1,0:T(8,128)(2,1)}), bf16[128,16,2048]{2,1,0:T(8,128)(2,1)}, u32[]{:S(2)}, u32[]{:S(2)}) async-start(bf16[128,16,2048]{2,1,0:T(8,128)(2,1)} %bitcast.217), calls=%async_computation | async-start | bytes 16777216 | tf_op jit(solution)/shard_map/all_to_all | solution.py:91
  214.3 22.8 %fusion.2 = f32[128,16,768]{2,0,1:T(8,128)} fusion(bf16[128,16,2048]{2,1,0:T(8,128)(2,1)} %all-to-all-done.2, bf16[1,2048,768]{2,1,0:T(8,128)(2,1)} %param.22), kind=kOutput, calls=%fused_computation.8 | convolution fusion | flops 6442450944 | bytes 17825792 | tf_op jit(solution)/shard_map/secd,edf->secf/dot_general | solution.py:94
  237.1 26.4 %convolution_convert_fusion.2 = bf16[128,16,2048]{2,0,1:T(8,128)(2,1)} fusion(bf16[1,768,2048]{2,1,0:T(8,128)(2,1)S(1)} %copy-done, f32[128,16,768]{2,0,1:T(8,128)} %fusion.2, bf16[128,16,2048]{2,1,0:T(8,128)(2,1)} %all-to-all-done.2, bf16[1,2048,768]{2,1,0:T(8,128)(2,1)} %param.21), kind=kOutput, calls=%fused_computation.30 | convolution fusion | flops 12898533376 | bytes 29360128 | tf_op jit(solution)/shard_map/secf,efd->secd/dot_general | solution.py:96
  263.5 11.2 %copy.84 = bf16[128,16,2048]{2,1,0:T(8,128)(2,1)} copy(bf16[128,16,2048]{2,0,1:T(8,128)(2,1)} %convolution_convert_fusion.2) | data formatting | bytes 16777216 | tf_op jit(solution)/shard_map/convert_element_type | solution.py:96
  274.7 60.7 %all-to-all-done = bf16[128,16,2048]{2,1,0:T(8,128)(2,1)} async-done(((bf16[128,16,2048]{2,1,0:T(8,128)(2,1)}), bf16[128,16,2048]{2,1,0:T(8,128)(2,1)}, u32[]{:S(2)}, u32[]{:S(2)}) %all-to-all-start) | async-done | bytes 8388640 | tf_op jit(solution)/shard_map/all_to_all | solution.py:91
  335.5 22.4 %all-to-all-start.3 = ((bf16[128,16,2048]{2,1,0:T(8,128)(2,1)}), bf16[128,16,2048]{2,1,0:T(8,128)(2,1)}, u32[]{:S(2)}, u32[]{:S(2)}) async-start(bf16[128,16,2048]{2,1,0:T(8,128)(2,1)} %copy.84), calls=%async_computation.3 | async-start | bytes 16777216 | tf_op jit(solution)/shard_map/all_to_all | solution.py:97
  357.8 22.8 %fusion.6 = f32[128,16,768]{2,0,1:T(8,128)} fusion(bf16[128,16,2048]{2,1,0:T(8,128)(2,1)} %all-to-all-done, bf16[1,2048,768]{2,1,0:T(8,128)(2,1)} %param.22), kind=kOutput, calls=%fused_computation.12 | convolution fusion | flops 6442450944 | bytes 17825792 | tf_op jit(solution)/shard_map/secd,edf->secf/dot_general | solution.py:94
  380.6 26.1 %convolution_convert_fusion.3 = bf16[128,16,2048]{2,0,1:T(8,128)(2,1)} fusion(bf16[1,768,2048]{2,1,0:T(8,128)(2,1)S(1)} %copy-done, f32[128,16,768]{2,0,1:T(8,128)} %fusion.6, bf16[128,16,2048]{2,1,0:T(8,128)(2,1)} %all-to-all-done, bf16[1,2048,768]{2,1,0:T(8,128)(2,1)} %param.21), kind=kOutput, calls=%fused_computation.31 | convolution fusion | flops 12898533376 | bytes 29360128 | tf_op jit(solution)/shard_map/secf,efd->secd/dot_general | solution.py:96
  406.7 11.2 %copy.75 = bf16[128,16,2048]{2,1,0:T(8,128)(2,1)} copy(bf16[128,16,2048]{2,0,1:T(8,128)(2,1)} %convolution_convert_fusion.3) | data formatting | bytes 16777216 | tf_op jit(solution)/shard_map/convert_element_type | solution.py:96
  417.9 62.9 %all-to-all-done.3 = bf16[128,16,2048]{2,1,0:T(8,128)(2,1)} async-done(((bf16[128,16,2048]{2,1,0:T(8,128)(2,1)}), bf16[128,16,2048]{2,1,0:T(8,128)(2,1)}, u32[]{:S(2)}, u32[]{:S(2)}) %all-to-all-start.3) | async-done | bytes 8388640 | tf_op jit(solution)/shard_map/all_to_all | solution.py:97
  480.9 6.3 %all-to-all-start.1 = ((bf16[128,16,2048]{2,1,0:T(8,128)(2,1)}), bf16[128,16,2048]{2,1,0:T(8,128)(2,1)}, u32[]{:S(2)}, u32[]{:S(2)}) async-start(bf16[128,16,2048]{2,1,0:T(8,128)(2,1)} %copy.75), calls=%async_computation.1 | async-start | bytes 16777216 | tf_op jit(solution)/shard_map/all_to_all | solution.py:97
  487.6 33.4 %select_reduce_fusion = bf16[3,128,2048]{2,1,0:T(8,128)(2,1)S(1)} fusion(pred[128,8,2048]{2,1,0:T(8,128)(4,1)} %get-tuple-element.16, bf16[3,128,8]{2,1,0:T(8,128)(2,1)S(1)} %copy.81), kind=kLoop, calls=%fused_computation.2 | loop fusion | flops 11796480 | bytes 3676160 | tf_op jit(solution)/shard_map/reduce_sum | solution.py:67
  520.9 34.6 %select_reduce_fusion.1 = bf16[3,128,2048]{2,1,0:T(8,128)(2,1)} fusion(pred[128,8,2048]{2,1,0:T(8,128)(4,1)} %get-tuple-element.14, bf16[3,128,8]{2,1,0:T(8,128)(2,1)S(1)} %copy.72), kind=kLoop, calls=%fused_computation.3 | loop fusion | flops 11796480 | bytes 3676160 | tf_op jit(solution)/shard_map/reduce_sum | solution.py:67
  555.5 5.9 fusion.148
  562.6 47.7 %all-to-all-done.1 = bf16[128,16,2048]{2,1,0:T(8,128)(2,1)} async-done(((bf16[128,16,2048]{2,1,0:T(8,128)(2,1)}), bf16[128,16,2048]{2,1,0:T(8,128)(2,1)}, u32[]{:S(2)}, u32[]{:S(2)}) %all-to-all-start.1) | async-done | bytes 8388640 | tf_op jit(solution)/shard_map/all_to_all | solution.py:97
  610.2 6.4 %fusion.147 = f32[384,2048]{1,0:T(8,128)S(1)} fusion(bf16[384,2048]{1,0:T(8,128)(2,1)} %bitcast.220, bf16[2048,2048]{1,0:T(8,128)(2,1)} %bitcast.25), kind=kOutput, calls=%fused_computation.158 | convolution fusion | flops 3221225472 | bytes 13107200 | tf_op jit(solution)/shard_map/dot_general | solution.py:68
  (57 shorter events, 23.0 us)
Async XLA Ops:
  0.0 237.1 %copy-start = (bf16[1,768,2048]{2,1,0:T(8,128)(2,1)S(1)}, bf16[1,768,2048]{2,1,0:T(8,128)(2,1)}, u32[]{:S(2)}) copy-start(bf16[1,768,2048]{2,1,0:T(8,128)(2,1)} %param.23) | copy-start | bytes 9437188
  1.7 11.7 %copy-start.9 = (f32[2048]{0:T(1024)S(1)}, f32[2048]{0:T(1024)}, u32[]{:S(2)}) copy-start(f32[2048]{0:T(1024)} %param.19) | copy-start | bytes 24580
  13.4 8.5 %copy-start.1 = (bf16[2,1,128,2048]{3,2,1,0:T(8,128)(2,1)S(1)}, bf16[2,1,128,2048]{3,2,1,0:T(8,128)(2,1)}, u32[]{:S(2)}) copy-start(bf16[2,1,128,2048]{3,2,1,0:T(8,128)(2,1)} %param.12) | copy-start | bytes 3145732
  21.9 8.7 %copy-start.7 = (bf16[16,32,8,128]{3,2,1,0:T(8,128)(2,1)}, bf16[16,32,8,128]{3,2,1,0:T(8,128)(2,1)S(1)}, u32[]{:S(2)}) copy-start(bf16[16,32,8,128]{3,2,1,0:T(8,128)(2,1)S(1)} %fusion.53) | copy-start | bytes 3145732
  30.6 1.0 copy-start.8
  31.6 4.7 copy-start.13
  45.9 8.6 %copy-start.11 = (f32[2048]{0:T(1024)S(1)}, f32[2048]{0:T(1024)}, u32[]{:S(2)}) copy-start(f32[2048]{0:T(1024)} %param.20) | copy-start | bytes 24580
  54.5 5.7 copy-start.3
  60.2 132.4 %all-to-all-start.2 = ((bf16[128,16,2048]{2,1,0:T(8,128)(2,1)}), bf16[128,16,2048]{2,1,0:T(8,128)(2,1)}, u32[]{:S(2)}, u32[]{:S(2)}) async-start(bf16[128,16,2048]{2,1,0:T(8,128)(2,1)} %bitcast.216), calls=%async_computation.2 | async-start | bytes 16777216 | tf_op jit(solution)/shard_map/all_to_all | solution.py:91
  84.4 9.5 %copy-start.2 = (bf16[2,1,128,2048]{3,2,1,0:T(8,128)(2,1)S(1)}, bf16[2,1,128,2048]{3,2,1,0:T(8,128)(2,1)}, u32[]{:S(2)}) copy-start(bf16[2,1,128,2048]{3,2,1,0:T(8,128)(2,1)} %param.12) | copy-start | bytes 3145732
  121.6 5.0 copy-start.5
  192.6 142.9 %all-to-all-start = ((bf16[128,16,2048]{2,1,0:T(8,128)(2,1)}), bf16[128,16,2048]{2,1,0:T(8,128)(2,1)}, u32[]{:S(2)}, u32[]{:S(2)}) async-start(bf16[128,16,2048]{2,1,0:T(8,128)(2,1)} %bitcast.217), calls=%async_computation | async-start | bytes 16777216 | tf_op jit(solution)/shard_map/all_to_all | solution.py:91
  335.5 145.4 %all-to-all-start.3 = ((bf16[128,16,2048]{2,1,0:T(8,128)(2,1)}), bf16[128,16,2048]{2,1,0:T(8,128)(2,1)}, u32[]{:S(2)}, u32[]{:S(2)}) async-start(bf16[128,16,2048]{2,1,0:T(8,128)(2,1)} %copy.84), calls=%async_computation.3 | async-start | bytes 16777216 | tf_op jit(solution)/shard_map/all_to_all | solution.py:97
  417.9 69.3 %copy-start.12 = (f32[2,1,128,8]{2,3,1,0:T(8,128)S(1)}, f32[2,1,128,8]{2,3,1,0:T(8,128)}, u32[]{:S(2)}) copy-start(f32[2,1,128,8]{2,3,1,0:T(8,128)} %param.14) | copy-start | bytes 24580
  480.9 129.4 %all-to-all-start.1 = ((bf16[128,16,2048]{2,1,0:T(8,128)(2,1)}), bf16[128,16,2048]{2,1,0:T(8,128)(2,1)}, u32[]{:S(2)}, u32[]{:S(2)}) async-start(bf16[128,16,2048]{2,1,0:T(8,128)(2,1)} %copy.75), calls=%async_computation.1 | async-start | bytes 16777216 | tf_op jit(solution)/shard_map/all_to_all | solution.py:97
  555.5 6.0 copy-start.4
  610.2 6.4 %copy-start.6 = (f32[128,2048]{1,0:T(8,128)S(1)}, f32[128,2048]{1,0:T(8,128)}, u32[]{:S(2)}) copy-start(f32[128,2048]{1,0:T(8,128)} %copy-done.5) | copy-start | bytes 3145732
  610.2 6.7 %copy-start.10 = (bf16[1,1,128,2048]{3,2,1,0:T(8,128)(2,1)S(1)}, bf16[1,1,128,2048]{3,2,1,0:T(8,128)(2,1)}, u32[]{:S(2)}) copy-start(bf16[1,1,128,2048]{3,2,1,0:T(8,128)(2,1)} %fusion.83) | copy-start | bytes 1572868
where the time goes:
time: 627 us; the launch traced here: 618 us
  waiting for transfers between devices  232 us (37%)
  matrix products  212 us (34%)
  other arithmetic  83.3 us (13%)
  starting transfers between devices  61.6 us (10%)
  local copies, waits for them, and re-layouts  29 us (5%)
    all_to_all x2, waiting for transfers between devices, local(): lax.all_to_all(buf.reshape(ep, el * cap, d), ep_axes, 0, 0, tiled=True)  121 us
    all_to_all x2, waiting for transfers between devices, local(): lax.all_to_all(out.reshape(ep, el * cap, d), ep_axes, 0, 0, tiled=True)  111 us
    reduce_sum x2, other arithmetic, combine(): jnp.sum(jnp.where(hit[None], pieces[..., None], jnp.zeros((), jnp.bfloat1...  68 us
    dot_general x6, matrix products, proj(): a = jnp.dot(u, w, preferred_element_type=jnp.float32).astype(jnp.bfloat16)  54.7 us
    dot_general x2, matrix products, local(): jnp.einsum('secf,efd->secd', act, w2, preferred_element_type=jnp.float32)  52.5 us
    dot_general x2, matrix products, local(): jnp.einsum('secd,edf->secf', recv, w3, preferred_element_type=jnp.float32)  45.6 us
    all_to_all x2, starting transfers between devices, local(): lax.all_to_all(buf.reshape(ep, el * cap, d), ep_axes, 0, 0, tiled=True)  33 us
    all_to_all x2, starting transfers between devices, local(): lax.all_to_all(out.reshape(ep, el * cap, d), ep_axes, 0, 0, tiled=True)  28.7 us
  transfers between devices with their start and end apart: 4, of which 4 were waited for; matrix products, arithmetic and copies ran while one was open for 41% of the time, Pallas kernels for 0%

commit v1 on v0

v1 whole, which is shorter than its diff:
```python
import functools

import jax
import jax.numpy as jnp
from jax import lax
from jax.experimental import pallas as pl
from jax.experimental.pallas import tpu as pltpu
from jax.sharding import PartitionSpec as P

HEAD = 128
VMEM_LIMIT = 67_000_000
MESH = pl.DeviceIdType.MESH
BF = jnp.bfloat16
F32 = jnp.float32
RING = 4
CORES = 2
COEF = {"z": 16, "y": 4, "x": 1}
PARTS = (("x", "y", "z"), ("y", "z", "x"), ("z", "x", "y"))
TILES = CORES * RING


def widths(d):
    lanes = d // 128
    base = lanes // 3
    return (base * 128, base * 128, (lanes - 2 * base) * 128)


class Sems:
    def __init__(self):
        self.n = 0

    def take(self, k=1):
        self.n += k
        return self.n - k


def moe_kernel(dims, nsem, z_hbm, h_ref, idx_ref, gate_ref, w1_hbm, w3_hbm, w2_hbm,
               y_ref, *rest):
    T, D, FF, CAP, TOP, COLS = dims
    it = iter(rest)
    recv = [next(it) for _ in range(3)]
    outp = [next(it) for _ in range(3)]
    ptr = [next(it) for _ in range(3)]
    r1 = [next(it) for _ in range(3)]
    r1t = [next(it) for _ in range(3)]
    r2 = [next(it) for _ in range(3)]
    r2t = [next(it) for _ in range(3)]
    ag = [next(it) for _ in range(3)]
    sbuf = [next(it) for _ in range(3)]
    mi = next(it)
    mg = next(it)
    lst = [next(it) for _ in range(3)]
    w1, w3, w2, xbuf, obuf = (next(it) for _ in range(5))
    stage = next(it)
    part_acc = [next(it) for _ in range(3)]
    q1 = [next(it) for _ in range(3)]
    q2 = [next(it) for _ in range(3)]
    hbuf = next(it)
    ssem, rsem = next(it), next(it)
    xsem, osem, lsem = next(it), next(it), next(it)

    c = lax.axis_index("row")
    q = lax.axis_index("col")
    pos = {"z": q // 16, "y": (q // 4) % 4, "x": q % 4}
    S, R = Sems(), Sems()
    pending = {}
    offs = (0, COLS[0], COLS[0] + COLS[1])

    def rel(v, s):
        return (v + s + RING) % RING

    def nb(dim, s, core=None):
        v = dict(pos)
        v[dim] = rel(v[dim], s)
        return {"row": c if core is None else core, "col": v["z"] * 16 + v["y"] * 4 + v["x"]}

    def send(src, dst, dev, si, ri):
        cp = pltpu.make_async_remote_copy(src_ref=src, dst_ref=dst, send_sem=ssem.at[si], recv_sem=rsem.at[ri],
                                          device_id=dev, device_id_type=MESH)
        cp.start()
        pending[id(cp)] = cp
        return cp

    def wait_in(ref, ri, dev):
        pltpu.make_async_remote_copy(src_ref=ref, dst_ref=ref, send_sem=ssem.at[0], recv_sem=rsem.at[ri],
                                     device_id=dev, device_id_type=MESH).wait_recv()

    barrier = pltpu.get_barrier_semaphore()
    friends = [nb(d, s, core) for d in "xyz" for s in (1, -1) for core in (c, 1 - c)]
    friends.append({"row": 1 - c, "col": q})
    for f in friends:
        pl.semaphore_signal(barrier, inc=1, device_id=f, device_id_type=MESH)
    wload = []
    for i, (a, b) in enumerate(((w1_hbm, w1), (w3_hbm, w3), (w2_hbm, w2))):
        cp = pltpu.make_async_copy(a.at[0], b, lsem.at[i])
        cp.start()
        wload.append(cp)
    own = {}
    for m in range(2):
        for p, (d1, d2, d3) in enumerate(PARTS):
            cp = pltpu.make_async_copy(z_hbm.at[m, :, pl.ds(offs[p], COLS[p])], ag[p].at[m, pos[d2], pos[d1]],
                                       lsem.at[3 + m * 3 + p])
            cp.start()
            own[m, p] = cp
    for p, (d1, d2, d3) in enumerate(PARTS):
        mi[p, pos[d2], pos[d1]] = idx_ref[...]
        mg[p, pos[d1]] = gate_ref[...]
    pl.semaphore_wait(barrier, len(friends))

    def ring1(dim, block):
        me = pos[dim]
        a = send(block(me, None), block(me, None), nb(dim, 1), S.take(), R.take())
        b = send(block(me, None), block(me, None), nb(dim, -1), S.take(), R.take())
        return a, b

    def ring2(dim, block, ab):
        me = pos[dim]
        ab[0].wait_recv()
        a = send(block(rel(me, -1), 0), block(rel(me, -1), 0), nb(dim, 1), S.take(), R.take())
        ab[1].wait_recv()
        b = send(block(rel(me, 1), 1), block(rel(me, 1), 1), nb(dim, -1), S.take(), R.take())
        return a, b

    def ring3(ab):
        ab[0].wait_recv()
        ab[1].wait_recv()

    def blk1(m, p):
        d2 = PARTS[p][1]

        def f(i, half):
            if half is None:
                return ag[p].at[m, pos[d2], i]
            return ag[p].at[m, pos[d2], i, pl.ds(half * (T // 2), T // 2)]
        return f

    def blk2(m, p):
        def f(i, half):
            if half is None:
                return ag[p].at[m, i]
            return ag[p].at[m, i, pl.ds(half * 2, 2)]
        return f

    def mi1(p):
        d2 = PARTS[p][1]

        def f(i, half):
            if half is None:
                return mi.at[p, pos[d2], i]
            return mi.at[p, pos[d2], i, half]
        return f

    def mg1(p):
        def f(i, half):
            if half is None:
                return mg.at[p, i]
            return mg.at[p, i, half]
        return f

    def mi2(p):
        def f(i, half):
            if half is None:
                return mi.at[p, i]
            return mi.at[p, i, pl.ds(half * 2, 2)]
        return f

    P3 = range(3)
    mim = [ring1(PARTS[p][0], mi1(p)) for p in P3]
    mgm = [ring1(PARTS[p][0], mg1(p)) for p in P3]
    s1 = {}
    for m in range(2):
        for p in P3:
            own[m, p].wait()
            s1[m, p] = ring1(PARTS[p][0], blk1(m, p))
    mim = [ring2(PARTS[p][0], mi1(p), mim[p]) for p in P3]
    mgm = [ring2(PARTS[p][0], mg1(p), mgm[p]) for p in P3]
    for m in range(2):
        for p in P3:
            s1[m, p] = ring2(PARTS[p][0], blk1(m, p), s1[m, p])
    for p in P3:
        ring3(mim[p])
        ring3(mgm[p])
    mim = [ring1(PARTS[p][1], mi2(p)) for p in P3]
    for m in range(2):
        for p in P3:
            ring3(s1[m, p])
            s1[m, p] = ring1(PARTS[p][1], blk2(m, p))
    mim = [ring2(PARTS[p][1], mi2(p), mim[p]) for p in P3]
    for m in range(2):
        for p in P3:
            s1[m, p] = ring2(PARTS[p][1], blk2(m, p), s1[m, p])
    for p in P3:
        ring3(mim[p])

    before = (lax.broadcasted_iota(jnp.int32, (T, T), 0) < lax.broadcasted_iota(jnp.int32, (T, T), 1)).astype(BF)

    def hits(rows, e, idx, gate):
        hit = jnp.zeros((rows, T), F32)
        g = jnp.zeros((rows, T), F32)
        for j in range(TOP):
            eq = jnp.broadcast_to(idx[j:j + 1, :], (rows, T)) == e
            hit = jnp.where(eq, 1.0, hit)
            if gate is not None:
                g = jnp.where(eq, jnp.broadcast_to(gate[j:j + 1, :], (rows, T)), g)
        return hit, g

    def ranks(hit):
        cum = jnp.dot(hit.astype(BF), before, preferred_element_type=F32)
        return jnp.where(hit > 0.0, cum, -1.0)

    def spread(rank, rows):
        slot = lax.broadcasted_iota(jnp.int32, (rows, CAP, T), 1).astype(F32)
        return jnp.broadcast_to(rank[:, None, :], (rows, CAP, T)) == slot

    def build(m, p):
        d1, d2, d3 = PARTS[p]
        r = lax.broadcasted_iota(jnp.int32, (2 * RING, T), 0)
        e = (r % 2) * 64 + COEF[d3] * ((pos[d3] + r // 2) % RING) + COEF[d2] * pos[d2] + COEF[d1] * pos[d1]

        def table(s, _):
            hit, _g = hits(2 * RING, e, mi[p, s // 4, s % 4, m], None)
            hbuf[s] = hit
            return 0

        lax.fori_loop(0, 16, table, 0)
        rk = ranks(hbuf[...].reshape(16 * 8, T))
        hbuf[...] = rk.reshape(16, 8, T)

        def one(s, _):
            sel = jnp.where(spread(hbuf[s], 8), 1.0, 0.0).reshape(8 * CAP, T).astype(BF)
            rows = jnp.dot(sel, ag[p][m, s // 4, s % 4], preferred_element_type=F32).astype(BF)
            rows = rows.reshape(8, CAP, COLS[p])
            if p == 2:
                sbuf[p][:, s % 4, s // 4] = rows
            else:
                sbuf[p][:, s // 4, s % 4] = rows
            return 0

        lax.fori_loop(0, 16, one, 0)

    def plane(ref, p, core, t):
        if p == 0:
            return ref.at[core, t]
        if p == 1:
            return ref.at[core, :, :, t]
        return ref.at[core, :, t]

    def x_start(p, src, dst, transit):
        dim = PARTS[p][2]
        me = pos[dim]
        st = {}
        st["t"] = (send(src(2, 0), transit.at[0], nb(dim, 1), S.take(), R.take()),
                   send(src(2, 1), transit.at[1], nb(dim, -1), S.take(), R.take()))
        st["l"], st["r"], st["o"], st["d"] = R.take(2), R.take(2), R.take(2), R.take()
        st["s"] = []
        for core in range(2):
            st["s"].append(send(src(1, core), dst(me, c), nb(dim, 1, core), S.take(), st["l"] + c))
            st["s"].append(send(src(3, core), dst(me, c), nb(dim, -1, core), S.take(), st["r"] + c))
        st["s"].append(send(src(0, 1 - c), dst(me, c), {"row": 1 - c, "col": q}, S.take(), st["d"]))
        st["s"].extend(st["t"])
        return st

    def x_forward(p, dst, transit, st):
        dim = PARTS[p][2]
        me = pos[dim]
        st["t"][0].wait_recv()
        send(transit.at[0], dst(rel(me, -1), c), nb(dim, 1, 0), S.take(), st["o"] + c)
        st["t"][1].wait_recv()
        send(transit.at[1], dst(rel(me, 1), c), nb(dim, -1, 1), S.take(), st["o"] + c)

    def x_wait(p, dst, st):
        dim = PARTS[p][2]
        me = pos[dim]
        for core in range(2):
            wait_in(dst(rel(me, -1), core), st["l"] + core, nb(dim, -1, core))
            wait_in(dst(rel(me, 1), core), st["r"] + core, nb(dim, 1, core))
            wait_in(dst(rel(me, 2), core), st["o"] + core, nb(dim, 1, core))
        wait_in(dst(me, 1 - c), st["d"], {"row": 1 - c, "col": q})

    def p_src(m, p):
        return lambda k, core: sbuf[p].at[2 * k + core]

    def p_dst(m, p):
        return lambda d3v, core: plane(recv[p].at[m], p, core, d3v)

    def r_src(m, p):
        return lambda k, core: plane(outp[p].at[m], p, core, rel(pos[PARTS[p][2]], k))

    def r_dst(m, p):
        return lambda d3v, core: r1[p].at[m, d3v, core]

    pst, loc = {}, {}

    def dispatch(m):
        for p in P3:
            ring3(s1[m, p])
            if m == 1:
                for cp in pst[0, p]["s"]:
                    cp.wait_send()
                    del pending[id(cp)]
                loc[0, p].wait()
            build(m, p)
            pst[m, p] = x_start(p, p_src(m, p), p_dst(m, p), ptr[p].at[m])
            cp = pltpu.make_async_copy(sbuf[p].at[c], p_dst(m, p)(pos[PARTS[p][2]], c), lsem.at[9 + m * 3 + p])
            cp.start()
            loc[m, p] = cp

    def p_forward(m):
        for p in P3:
            x_forward(p, p_dst(m, p), ptr[p].at[m], pst[m, p])

    def p_wait(m):
        for p in P3:
            x_wait(p, p_dst(m, p), pst[m, p])
            if m == 1:
                loc[m, p].wait()

    rows_t = RING * RING * CAP

    def xload(m, i, slot):
        return [pltpu.make_async_copy(recv[p].at[m, i // 4, i % 4], xbuf.at[slot, :, :, :, pl.ds(offs[p], COLS[p])],
                                      xsem.at[slot, p]) for p in P3]

    def ostore(m, i, slot):
        return [pltpu.make_async_copy(obuf.at[slot, :, :, :, pl.ds(offs[p], COLS[p])], outp[p].at[m, i // 4, i % 4],
                                      osem.at[slot, p]) for p in P3]

    def expert(m, lo, hi):
        if lo == 0:
            for cp in xload(m, 0, 0):
                cp.start()

        def tile(i, _):
            slot = i % 2

            @pl.when(i + 1 < TILES)
            def _():
                for cp in xload(m, i + 1, (i + 1) % 2):
                    cp.start()

            for cp in xload(m, i, slot):
                cp.wait()

            @pl.when(i >= 2)
            def _():
                for cp in ostore(m, i - 2, slot):
                    cp.wait()

            xt = xbuf[slot].reshape(rows_t, D)
            h1 = jnp.dot(xt, w1[...], preferred_element_type=F32)
            h3 = jnp.dot(xt, w3[...], preferred_element_type=F32)
            act = (jax.nn.silu(h1) * h3).astype(BF)
            o = jnp.dot(act, w2[...], preferred_element_type=F32).astype(BF)
            obuf[slot] = o.reshape(RING, RING, CAP, D)
            for cp in ostore(m, i, slot):
                cp.start()
            return 0

        lax.fori_loop(lo, hi, tile, 0)
        if hi == TILES:
            for i in (TILES - 2, TILES - 1):
                for cp in ostore(m, i, i % 2):
                    cp.wait()

    rst = {}

    def r1_start(m):
        cps = []
        for p in P3:
            rst[m, p] = x_start(p, r_src(m, p), r_dst(m, p), r1t[p].at[m])
            cp = pltpu.make_async_copy(r_src(m, p)(0, c), lst[p], lsem.at[15 + p])
            cp.start()
            cps.append(cp)
        for p in P3:
            cps[p].wait()
            cp = pltpu.make_async_copy(lst[p], r_dst(m, p)(pos[PARTS[p][2]], c), lsem.at[15 + p])
            cp.start()
            cps[p] = cp
        for p in P3:
            cps[p].wait()

    def r1_forward(m):
        for p in P3:
            x_forward(p, r_dst(m, p), r1t[p].at[m], rst[m, p])

    def r1_for(m, p, t):
        return r1[p].at[m, :, :, :, t] if p == 2 else r1[p].at[m, :, :, t]

    def r1_half(m, p, t, half):
        hs = pl.ds(2 * half, 2)
        return r1[p].at[m, hs, :, :, t] if p == 2 else r1[p].at[m, hs, :, t]

    r2st = {}

    def r2_start(m):
        for p in P3:
            x_wait(p, r_dst(m, p), rst[m, p])
            dim = PARTS[p][1]
            me = pos[dim]
            st = {}
            st["t"] = (send(r1_half(m, p, rel(me, 2), 0), r2t[p].at[m, 0], nb(dim, 1), S.take(), R.take()),
                       send(r1_half(m, p, rel(me, 2), 1), r2t[p].at[m, 1], nb(dim, -1), S.take(), R.take()))
            st["n"] = (send(r1_for(m, p, rel(me, 1)), r2[p].at[m, me], nb(dim, 1), S.take(), R.take()),
                       send(r1_for(m, p, rel(me, -1)), r2[p].at[m, me], nb(dim, -1), S.take(), R.take()))
            r2st[m, p] = st

    def r2_forward(m):
        for p in P3:
            dim = PARTS[p][1]
            me = pos[dim]
            st = r2st[m, p]
            st["t"][0].wait_recv()
            a = send(r2t[p].at[m, 0], r2[p].at[m, rel(me, -1), pl.ds(0, 2)], nb(dim, 1), S.take(), R.take())
            st["t"][1].wait_recv()
            b = send(r2t[p].at[m, 1], r2[p].at[m, rel(me, 1), pl.ds(2, 2)], nb(dim, -1), S.take(), R.take())
            st["f"] = (a, b)

    def r2_wait(m, p):
        st = r2st[m, p]
        for cp in st["n"] + st["f"]:
            cp.wait_recv()

    def stage_in(m, p, k, slot):
        d1, d2, d3 = PARTS[p]
        s1v = rel(pos[d1], k)
        cols = pl.ds(0, COLS[p])
        mine = r1[p].at[m, :, :, s1v, pos[d2]] if p == 2 else r1[p].at[m, :, :, pos[d2], s1v]
        cps = [pltpu.make_async_copy(mine, stage.at[slot, 0, :, :, :, cols], xsem.at[2 + slot, 0])]
        for j in range(1, RING):
            cps.append(pltpu.make_async_copy(r2[p].at[m, rel(pos[d2], j), :, :, s1v], stage.at[slot, j, :, :, :, cols],
                                             xsem.at[2 + slot, j]))
        return cps

    def combine(m, p):
        d1, d2, d3 = PARTS[p]
        n_e = 8 * RING
        r = lax.broadcasted_iota(jnp.int32, (n_e, T), 0)
        e = (r % 2) * 64 + COEF[d3] * ((r // 2) % RING) + COEF[d2] * ((pos[d2] + r // 8) % RING) + COEF[d1] * pos[d1]
        cps = stage_in(m, p, 0, 0)
        for cp in cps:
            cp.start()
        for k in range(RING):
            s1v = rel(pos[d1], k)
            nxt = None
            if k + 1 < RING:
                nxt = stage_in(m, p, k + 1, (k + 1) % 2)
                for cp in nxt:
                    cp.start()
            hit, g = hits(n_e, e, mi[p, pos[d2], s1v, m], mg[p, s1v, m])
            mask = spread(ranks(hit), n_e)
            for cp in cps:
                cp.wait()
            cps = nxt
            rows = stage[k % 2, :, :, :, :, 0:COLS[p]].reshape(n_e * CAP, COLS[p])
            acc = jnp.zeros((T, COLS[p]), F32)
            rest_g = g
            for _ in range(3):
                piece = rest_g.astype(BF).astype(F32)
                rest_g = rest_g - piece
                wt = jnp.where(mask, jnp.broadcast_to(piece[:, None, :], (n_e, CAP, T)), 0.0)
                wt = wt.reshape(n_e * CAP, T).astype(BF)
                acc = acc + lax.dot_general(wt, rows, (((0,), (0,)), ((), ())), preferred_element_type=F32)
            part_acc[p][k] = acc

    r3 = {}

    def r3_one(m, p):
        dim = PARTS[p][0]
        half = T // 2
        a = send(part_acc[p].at[2, pl.ds(0, half)], q1[p].at[m, 0], nb(dim, 1), S.take(), R.take())
        b = send(part_acc[p].at[2, pl.ds(half, half)], q1[p].at[m, 1], nb(dim, -1), S.take(), R.take())
        r3[m, p] = [a, b]

    def r3_two(m, p):
        dim = PARTS[p][0]
        half = T // 2
        a, b = r3[m, p]
        a.wait_recv()
        part_acc[p][1, 0:half] = part_acc[p][1, 0:half] + q1[p][m, 0]
        a2 = send(part_acc[p].at[1], q2[p].at[m, 0], nb(dim, 1), S.take(), R.take())
        b.wait_recv()
        part_acc[p][3, half:T] = part_acc[p][3, half:T] + q1[p][m, 1]
        b2 = send(part_acc[p].at[3], q2[p].at[m, 1], nb(dim, -1), S.take(), R.take())
        r3[m, p] += [a2, b2]

    def r3_end(m, p):
        for cp in r3[m, p][2:]:
            cp.wait_recv()
        cols = slice(offs[p], offs[p] + COLS[p])
        acc = part_acc[p][0] + q2[p][m, 0] + q2[p][m, 1]
        y_ref[m, :, cols] = (h_ref[m, :, cols].astype(F32) + acc).astype(BF)
        for cp in r3[m, p]:
            cp.wait_send()
            del pending[id(cp)]

    dispatch(0)
    p_forward(0)
    dispatch(1)
    p_wait(0)
    for cp in wload:
        cp.wait()
    expert(0, 0, 4)
    p_forward(1)
    expert(0, 4, 8)
    r1_start(0)
    p_wait(1)
    expert(1, 0, 4)
    r1_forward(0)
    expert(1, 4, 8)
    r1_start(1)
    r2_start(0)
    r1_forward(1)
    r2_forward(0)
    r2_start(1)
    for p in P3:
        r2_wait(0, p)
        combine(0, p)
        r3_one(0, p)
    r2_forward(1)
    for p in P3:
        r3_two(0, p)
    for p in P3:
        r3_end(0, p)
    for p in P3:
        r2_wait(1, p)
        combine(1, p)
        r3_one(1, p)
    for p in P3:
        r3_two(1, p)
    for p in P3:
        r3_end(1, p)
    for cp in list(pending.values()):
        cp.wait_send()
    if S.n > nsem or R.n > nsem:
        raise ValueError(f"{S.n} {R.n}")


NSEM = 260


def moe(z, h, idx, gates, w1, w3, w2, cap):
    _, T, D = z.shape
    FF = w1.shape[-1]
    TOP = idx.shape[1]
    COLS = widths(D)
    dims = (T, D, FF, cap, TOP, COLS)
    hbm = []
    for lead in ((2, 2, 4, 4, 4), (2, 2, 4, 4, 4), (2, 2, 4, 4), (2, 4, 2, 4, 4), (2, 2, 4, 4),
                 (2, 4, 4, 2, 4), (2, 2, 2, 2, 4)):
        for p in range(3):
            hbm.append(jax.ShapeDtypeStruct(lead + (cap, COLS[p]), BF))
    V = pltpu.VMEM
    scratch = [V((2, 4, 4, T, COLS[p]), BF) for p in range(3)]
    scratch += [V((8, 4, 4, cap, COLS[p]), BF) for p in range(3)]
    scratch += [V((3, 4, 4, 2, TOP, T), jnp.int32), V((3, 4, 2, TOP, T), F32)]
    scratch += [V((4, 4, cap, COLS[p]), BF) for p in range(3)]
    scratch += [V((D, FF), BF), V((D, FF), BF), V((FF, D), BF), V((2, 4, 4, cap, D), BF), V((2, 4, 4, cap, D), BF)]
    scratch += [V((2, 4, 4, 2, cap, max(COLS)), BF)]
    scratch += [V((4, T, COLS[p]), F32) for p in range(3)]
    scratch += [V((2, 2, T // 2, COLS[p]), F32) for p in range(3)]
    scratch += [V((2, 2, T, COLS[p]), F32) for p in range(3)]
    scratch += [V((16, 8, T), F32)]
    DMA = pltpu.SemaphoreType.DMA
    scratch += [DMA((NSEM,)), DMA((NSEM,)), DMA((4, 4)), DMA((2, 3)), DMA((18,))]
    any_spec = pl.BlockSpec(memory_space=pl.ANY)
    vm = pl.BlockSpec(memory_space=pltpu.VMEM)
    out = pl.pallas_call(
        functools.partial(moe_kernel, dims, NSEM),
        out_shape=[jax.ShapeDtypeStruct((2, T, D), BF)] + hbm,
        in_specs=[any_spec, vm, vm, vm, any_spec, any_spec, any_spec],
        out_specs=[vm] + [any_spec] * len(hbm),
        scratch_shapes=scratch,
        compiler_params=pltpu.CompilerParams(collective_id=0, has_side_effects=True, vmem_limit_bytes=VMEM_LIMIT),
    )(z, h, idx, gates, w1, w3, w2)
    return out[0]


def rms(v, g):
    vf = v.astype(jnp.float32)
    return (vf * lax.rsqrt(jnp.mean(vf * vf, axis=-1, keepdims=True) + 1e-6) * g).astype(jnp.bfloat16)


def attention(x, wq, wk, wv, wo, g):
    ns, seq, d = x.shape
    nh = wq.shape[1] // HEAD
    xf = x.reshape(ns * seq, d)
    u = rms(xf, g)

    def proj(w):
        a = jnp.dot(u, w, preferred_element_type=jnp.float32).astype(jnp.bfloat16)
        return a.reshape(ns, seq, nh, HEAD)

    q, k, v = proj(wq), proj(wk), proj(wv)
    causal = jnp.arange(seq)[:, None] >= jnp.arange(seq)[None, :]
    s = jnp.einsum("bqhe,bkhe->bhqk", q, k, preferred_element_type=jnp.float32) * HEAD ** -0.5
    s = jnp.where(causal, s, -1e30)
    p = jax.nn.softmax(s, axis=-1).astype(jnp.bfloat16)
    o = jnp.einsum("bhqk,bkhe->bqhe", p, v, preferred_element_type=jnp.float32).astype(jnp.bfloat16)
    o = o.reshape(ns * seq, nh * HEAD)
    a = jnp.dot(o, wo, preferred_element_type=jnp.float32)
    return (xf.astype(jnp.float32) + a).astype(jnp.bfloat16)


def capacity(t, top, n_exp):
    return ((top * ((2 * t + n_exp - 1) // n_exp) + 7) // 8) * 8


def solution(mesh):
    ep_axes = ("row", "col")
    tok_axes = ("dp", "row", "col")
    ep = mesh.shape["row"] * mesh.shape["col"]

    def local(x, idx, gates, wq, wk, wv, wo, gattn, gmoe, w1, w3, w2):
        seq, d = x.shape[2:]
        top = idx.shape[-1]
        cap = capacity(seq, top, ep)
        h = attention(x[:, 0], wq, wk, wv, wo, gattn)
        z = rms(h, gmoe)
        y = moe(z.reshape(2, seq, d), h.reshape(2, seq, d), jnp.swapaxes(idx[:, 0], 1, 2),
                jnp.swapaxes(gates[:, 0], 1, 2), w1, w3, w2, cap)
        return y[:, None]

    tok_spec = P(None, tok_axes)
    exp_spec = P(ep_axes)
    return jax.shard_map(local, mesh=mesh,
                         in_specs=(tok_spec, tok_spec, tok_spec, P(), P(), P(), P(), P(), P(), exp_spec, exp_spec, exp_spec),
                         out_specs=tok_spec, check_vma=False)
```

time: 627 us -> 372 us (0.59)
  the two profiles are of different devices: /device:TPU:3 before, /device:TPU:10 now
where the time goes in v1:
time: 372 us; the launch traced here: 366 us
  Pallas kernels  316 us (85%)
  matrix products  35.7 us (10%)
  local copies, waits for them, and re-layouts  8.42 us (2%)
  other arithmetic  5.58 us (2%)
    pallas_call x1, Pallas kernels, moe(): pl.pallas_call(functools.partial(moe_kernel, dims, NSEM), out_shape=[jax....  316 us
    dot_general x3, matrix products, proj(): a = jnp.dot(u, w, preferred_element_type=jnp.float32).astype(jnp.bfloat16)  21.7 us
    dot_general x1, matrix products, attention(): a = jnp.dot(o, wo, preferred_element_type=jnp.float32)  11.3 us

profile of v1, /device:TPU:10, one launch (start us, length us, event | category | flops | bytes accessed | tf_op | source)
XLA Modules:
  0.0 365.6 jit_solution(11360514268341819697)
XLA Ops:
  0.0 1.5 multiply_reduce_fusion
  1.5 0.0 slice-start
  1.6 1.7 fusion.10
  3.2 0.0 slice-start.1
  3.3 0.0 slice-start.2
  3.3 0.0 slice-start.3
  3.3 8.6 %fusion.23 = bf16[32,8,32,128]{3,1,2,0:T(8,128)(2,1)S(1)} fusion(bf16[256,2048]{1,0:T(8,128)(2,1)S(1)} %fusion.10, bf16[2048,4096]{1,0:T(8,128)(2,1)} %param.16), kind=kOutput, calls=%fused_computation.33 | convolution fusion | flops 4296015872 | bytes 19922944 | tf_op jit(solution)/shard_map/dot_general | solution.py:590
  11.9 0.5 copy.27
  12.3 0.0 slice-done
  12.3 0.0 slice-done.1
  12.4 0.0 slice-done.2
  12.4 0.4 slice-done.3
  12.8 4.7 %fusion.22 = bf16[32,8,32,128]{3,1,2,0:T(8,128)(2,1)S(1)} fusion(bf16[256,2048]{1,0:T(8,128)(2,1)S(1)} %fusion.10, bf16[2048,4096]{1,0:T(8,128)(2,1)S(1)} %bitcast.59), kind=kOutput, calls=%fused_computation.32 | convolution fusion | flops 4296015872 | bytes 19922944 | tf_op jit(solution)/shard_map/dot_general | solution.py:590
  17.5 0.5 copy.26
  18.0 1.4 fusion.12
  19.4 1.1 fusion.26
  20.5 8.4 %fusion.21 = bf16[32,8,32,128]{3,1,2,0:T(8,128)(2,1)S(1)} fusion(bf16[256,2048]{1,0:T(8,128)(2,1)S(1)} %fusion.10, bf16[2048,4096]{1,0:T(8,128)(2,1)} %param.17), kind=kOutput, calls=%fused_computation.31 | convolution fusion | flops 4296015872 | bytes 19922944 | tf_op jit(solution)/shard_map/dot_general | solution.py:590
  28.9 0.5 copy.25
  29.4 1.3 convert_bitcast_fusion
  30.6 0.0 copy-start
  30.6 3.2 copy.22
  33.8 0.0 copy-done
  33.9 0.0 copy-start.2
  33.9 11.3 %fusion.3 = (f32[256]{0:T(256)S(1)}, bf16[256,2048]{1,0:T(8,128)(2,1)S(1)}) fusion(bf16[4096,2048]{1,0:T(8,128)(2,1)} %param.18, bf16[32,8,32,128]{3,2,1,0:T(8,128)(2,1)} %bitcast.54, bf16[256,2048]{1,0:T(8,128)(2,1)S(1)} %bitcast.50), kind=kOutput, calls=%fused_computation.12 | convolution fusion | flops 4298113024 | bytes 20972544 | tf_op jit(solution)/shard_map/dot_general | solution.py:600
  45.2 0.0 copy-start.1
  45.2 1.0 copy-done.1
  46.3 0.0 copy-done.2
  46.3 1.3 fusion.5
  47.5 315.5 %shard_map.118 = (bf16[2,128,2048]{2,1,0:T(8,128)(2,1)}, bf16[2,2,4,4,4,16,640]{6,5,4,3,2,1,0:T(8,128)(2,1)}, bf16[2,2,4,4,4,16,640]{6,5,4,3,2,1,0:T(8,128)(2,1)...) custom-call(bf16[2,128,2048]{2,1,0:T(8,128)(2,1)} %bitcast.52, ...), custom_call_target="tpu_custom_call" | custom-call | tf_op jit(solution)/shard_map/pallas_call | solution.py:567
  363.1 2.3 copy.44
  (4 shorter events, 0.0 us)
Async XLA Ops:
  1.5 10.8 %slice-start = ((s8[16777216]{0:T(1024)(128)(4,1)}), s8[4194304]{0:T(1024)(128)(4,1)S(1)}, s32[]{:S(2)}) async-start(s8[16777216]{0:T(1024)(128)(4,1)} %bitcast.58), calls=%async_computation | async-start | bytes 8388608
  3.2 9.1 %slice-start.1 = ((s8[16777216]{0:T(1024)(128)(4,1)}), s8[4194304]{0:T(1024)(128)(4,1)S(1)}, s32[]{:S(2)}) async-start(s8[16777216]{0:T(1024)(128)(4,1)} %bitcast.58), calls=%async_computation.1 | async-start | bytes 8388608
  3.3 9.1 %slice-start.2 = ((s8[16777216]{0:T(1024)(128)(4,1)}), s8[4194304]{0:T(1024)(128)(4,1)S(1)}, s32[]{:S(2)}) async-start(s8[16777216]{0:T(1024)(128)(4,1)} %bitcast.58), calls=%async_computation.2 | async-start | bytes 8388608
  3.3 9.5 %slice-start.3 = ((s8[16777216]{0:T(1024)(128)(4,1)}), s8[4194304]{0:T(1024)(128)(4,1)S(1)}, s32[]{:S(2)}) async-start(s8[16777216]{0:T(1024)(128)(4,1)} %bitcast.58), calls=%async_computation.3 | async-start | bytes 8388608
  30.6 3.2 copy-start
  33.9 12.4 %copy-start.2 = (f32[2048]{0:T(1024)S(1)}, f32[2048]{0:T(1024)}, u32[]{:S(2)}) copy-start(f32[2048]{0:T(1024)} %param.20) | copy-start | bytes 24580
  45.2 1.1 copy-start.1

commit v2 on v1

v2 whole, which is shorter than its diff:
```python
import functools

import jax
import jax.numpy as jnp
from jax import lax
from jax.experimental import pallas as pl
from jax.experimental.pallas import tpu as pltpu
from jax.sharding import PartitionSpec as P

HEAD = 128
VMEM_LIMIT = 67_000_000
HEADS_PER_STEP = 2
ORDER = (
    "mt1", "a1_02", "a1_00", "a1_01", "mt2", "a1_11", "a1_10", "a2_00", "a2_02", "mt3", "a2_10", "a2_01", "a2_11",
    "mt4", "a1_12", "a3_02", "a3_00", "a3_11", "a2_12", "a3_10", "a3_01", "tab", "a4_02", "a4_00", "a3_12", "bd_02",
    "a4_01", "a4_10", "ps_02", "a4_11", "bd_00", "a4_12", "bd_01", "ps_00", "ps_01", "bd_11", "pf_02", "pf_01",
    "bd_10", "ps_11", "pf_00", "bd_12", "ps_12", "ps_10", "E0_0", "E0_1", "pf_10", "E0_2", "pf_11", "E0_3", "E0_4",
    "pf_12", "E0_5", "E0_6", "E0_7", "q1_01", "q1_02", "q1_00", "E1_0", "E1_1", "E1_2", "E1_3", "qf_01", "E1_4",
    "E1_5", "qf_02", "qf_00", "E1_6", "E1_7", "q1_11", "q1_10", "q1_12", "q2_02", "qf_10", "qf_11", "q2_01", "qf_12",
    "q2_10", "qg_10", "qg_02", "q2_12", "qg_01", "q2_11", "ca_02", "q2_00", "qg_00", "qg_12", "ca_10", "qg_11",
    "cb_02", "cb_10", "r3_02", "ca_01", "cb_01", "ca_11", "cb_11", "ca_12", "ca_00", "r3_01", "r3_10", "cb_12",
    "fin_02", "r3_12", "cb_00", "r3_00", "r3_11", "fin_10", "fin_01", "fin_12", "fin_11", "fin_00",
)


MESH = pl.DeviceIdType.MESH
BF = jnp.bfloat16
F32 = jnp.float32
RING = 4
CORES = 2
COEF = {"z": 16, "y": 4, "x": 1}
PARTS = (("x", "y", "z"), ("y", "z", "x"), ("z", "x", "y"))
TILES = CORES * RING


def widths(d):
    lanes = d // 128
    base = lanes // 3
    return (base * 128, base * 128, (lanes - 2 * base) * 128)


class Sems:
    def __init__(self):
        self.n = 0

    def take(self, k=1):
        self.n += k
        return self.n - k


def moe_kernel(dims, nsem, z_hbm, h_ref, idx_ref, gate_ref, w1_hbm, w3_hbm, w2_hbm,
               y_ref, *rest):
    T, D, FF, CAP, TOP, COLS = dims
    it = iter(rest)
    recv = [next(it) for _ in range(3)]
    outp = [next(it) for _ in range(3)]
    ptr = [next(it) for _ in range(3)]
    r1 = [next(it) for _ in range(3)]
    r1t = [next(it) for _ in range(3)]
    r2 = [next(it) for _ in range(3)]
    r2t = [next(it) for _ in range(3)]
    ag = [next(it) for _ in range(3)]
    mi = next(it)
    mg = next(it)
    lst = [next(it) for _ in range(3)]
    w1, w3, w2, xbuf, obuf = (next(it) for _ in range(5))
    stage = next(it)
    part_acc = [next(it) for _ in range(3)]
    q1 = [next(it) for _ in range(3)]
    q2 = [next(it) for _ in range(3)]
    drank = [next(it) for _ in range(3)]
    crank = [next(it) for _ in range(3)]
    cgate = [next(it) for _ in range(3)]
    ssem, rsem = next(it), next(it)
    xsem, osem, lsem, csem = next(it), next(it), next(it), next(it)

    c = lax.axis_index("row")
    q = lax.axis_index("col")
    pos = {"z": q // 16, "y": (q // 4) % 4, "x": q % 4}
    S, R = Sems(), Sems()
    pending = {}
    offs = (0, COLS[0], COLS[0] + COLS[1])

    def rel(v, s):
        return (v + s + RING) % RING

    def nb(dim, s, core=None):
        v = dict(pos)
        v[dim] = rel(v[dim], s)
        return {"row": c if core is None else core, "col": v["z"] * 16 + v["y"] * 4 + v["x"]}

    def make(src, dst, dev, si, ri):
        return pltpu.make_async_remote_copy(src_ref=src, dst_ref=dst, send_sem=ssem.at[si], recv_sem=rsem.at[ri],
                                            device_id=dev, device_id_type=MESH)

    def send(src, dst, dev, si, ri):
        cp = make(src, dst, dev, si, ri)
        cp.start()
        pending[id(cp)] = cp
        return cp

    def wait_in(ref, ri, dev):
        pltpu.make_async_remote_copy(src_ref=ref, dst_ref=ref, send_sem=ssem.at[0], recv_sem=rsem.at[ri],
                                     device_id=dev, device_id_type=MESH).wait_recv()

    barrier = pltpu.get_barrier_semaphore()
    friends = [nb(d, s, core) for d in "xyz" for s in (1, -1) for core in (c, 1 - c)]
    friends.append({"row": 1 - c, "col": q})
    for f in friends:
        pl.semaphore_signal(barrier, inc=1, device_id=f, device_id_type=MESH)
    wload = []
    for i, (a, b) in enumerate(((w1_hbm, w1), (w3_hbm, w3), (w2_hbm, w2))):
        cp = pltpu.make_async_copy(a.at[0], b, lsem.at[i])
        cp.start()
        wload.append(cp)
    own = {}
    for m in range(2):
        for p, (d1, d2, d3) in enumerate(PARTS):
            cp = pltpu.make_async_copy(z_hbm.at[m, :, pl.ds(offs[p], COLS[p])], ag[p].at[m, pos[d2], pos[d1]],
                                       lsem.at[3 + m * 3 + p])
            cp.start()
            own[m, p] = cp
    for p, (d1, d2, d3) in enumerate(PARTS):
        mi[p, pos[d2], pos[d1]] = idx_ref[...]
        mg[p, pos[d1]] = gate_ref[...]
    pl.semaphore_wait(barrier, len(friends))

    def ring1(dim, block):
        me = pos[dim]
        a = send(block(me, None), block(me, None), nb(dim, 1), S.take(), R.take())
        b = send(block(me, None), block(me, None), nb(dim, -1), S.take(), R.take())
        return a, b

    def ring2(dim, block, ab):
        me = pos[dim]
        ab[0].wait_recv()
        a = send(block(rel(me, -1), 0), block(rel(me, -1), 0), nb(dim, 1), S.take(), R.take())
        ab[1].wait_recv()
        b = send(block(rel(me, 1), 1), block(rel(me, 1), 1), nb(dim, -1), S.take(), R.take())
        return a, b

    def ring3(ab):
        ab[0].wait_recv()
        ab[1].wait_recv()

    def blk1(m, p):
        d2 = PARTS[p][1]

        def f(i, half):
            if half is None:
                return ag[p].at[m, pos[d2], i]
            return ag[p].at[m, pos[d2], i, pl.ds(half * (T // 2), T // 2)]
        return f

    def blk2(m, p):
        def f(i, half):
            if half is None:
                return ag[p].at[m, i]
            return ag[p].at[m, i, pl.ds(half * 2, 2)]
        return f

    def mi1(p):
        d2 = PARTS[p][1]

        def f(i, half):
            if half is None:
                return mi.at[p, pos[d2], i]
            return mi.at[p, pos[d2], i, half]
        return f

    def mg1(p):
        def f(i, half):
            if half is None:
                return mg.at[p, i]
            return mg.at[p, i, half]
        return f

    def mi2(p):
        def f(i, half):
            if half is None:
                return mi.at[p, i]
            return mi.at[p, i, pl.ds(half * 2, 2)]
        return f

    P3 = range(3)
    s1, asends = {}, {}

    def a_one(m, p):
        own[m, p].wait()
        s1[m, p] = ring1(PARTS[p][0], blk1(m, p))
        asends[m, p] = list(s1[m, p])

    def a_two(m, p):
        s1[m, p] = ring2(PARTS[p][0], blk1(m, p), s1[m, p])
        asends[m, p] += s1[m, p]

    def a_three(m, p):
        ring3(s1[m, p])
        s1[m, p] = ring1(PARTS[p][1], blk2(m, p))
        asends[m, p] += s1[m, p]

    def a_four(m, p):
        s1[m, p] = ring2(PARTS[p][1], blk2(m, p), s1[m, p])
        asends[m, p] += s1[m, p]

    before = (lax.broadcasted_iota(jnp.int32, (T, T), 0) < lax.broadcasted_iota(jnp.int32, (T, T), 1)).astype(BF)

    def hits(rows, e, idx, gate):
        hit = jnp.zeros((rows, T), F32)
        g = jnp.zeros((rows, T), F32)
        for j in range(TOP):
            eq = jnp.broadcast_to(idx[j:j + 1, :], (rows, T)) == e
            hit = jnp.where(eq, 1.0, hit)
            if gate is not None:
                g = jnp.where(eq, jnp.broadcast_to(gate[j:j + 1, :], (rows, T)), g)
        return hit, g

    def ranks(hit):
        cum = jnp.dot(hit.astype(BF), before, preferred_element_type=F32)
        return jnp.where(hit > 0.0, cum, -1.0)

    def spread(rank, rows):
        slot = lax.broadcasted_iota(jnp.int32, (rows, CAP, T), 1).astype(F32)
        return jnp.broadcast_to(rank[:, None, :], (rows, CAP, T)) == slot

    def tables(p):
        d1, d2, d3 = PARTS[p]
        r = lax.broadcasted_iota(jnp.int32, (2 * RING, T), 0)
        e = (r % 2) * 64 + COEF[d3] * ((pos[d3] + r // 2) % RING) + COEF[d2] * pos[d2] + COEF[d1] * pos[d1]

        def one(i, _):
            drank[p][i], _g = hits(2 * RING, e, mi[p, (i // 4) % 4, i % 4, i // 16], None)
            return 0

        lax.fori_loop(0, 32, one, 0)
        drank[p][...] = ranks(drank[p][...].reshape(32 * 8, T)).reshape(32, 8, T)
        n_e = 8 * RING
        r = lax.broadcasted_iota(jnp.int32, (n_e, T), 0)
        e = (r % 2) * 64 + COEF[d3] * ((r // 2) % RING) + COEF[d2] * ((pos[d2] + r // 8) % RING) + COEF[d1] * pos[d1]

        def two(i, _):
            s1v = (pos[d1] + i % 4) % RING
            hit, g = hits(n_e, e, mi[p, pos[d2], s1v, i // 4], mg[p, s1v, i // 4])
            crank[p][i] = ranks(hit)
            cgate[p][i] = g
            return 0

        lax.fori_loop(0, 8, two, 0)

    def build(m, p):
        for cp in asends.pop((m, p)):
            cp.wait_send()
            del pending[id(cp)]

        def one(s, _):
            sel = jnp.where(spread(drank[p][m * 16 + s], 8), 1.0, 0.0).reshape(8 * CAP, T).astype(BF)
            rows = jnp.dot(sel, ag[p][m, s // 4, s % 4], preferred_element_type=F32)
            ag[p][m, s // 4, s % 4] = rows.astype(BF)
            return 0

        lax.fori_loop(0, 16, one, 0)

    def plane(ref, p, core, t):
        if p == 0:
            return ref.at[core, t]
        if p == 1:
            return ref.at[core, :, :, t]
        return ref.at[core, t]

    def x_start(p, src, dst, transit):
        dim = PARTS[p][2]
        me = pos[dim]
        st = {}
        st["t"] = (send(src(2, 0), transit.at[0], nb(dim, 1), S.take(), R.take()),
                   send(src(2, 1), transit.at[1], nb(dim, -1), S.take(), R.take()))
        st["l"], st["r"], st["o"], st["d"] = R.take(2), R.take(2), R.take(2), R.take()
        st["f"] = (S.take(), S.take())
        for core in range(2):
            send(src(1, core), dst(me, c), nb(dim, 1, core), S.take(), st["l"] + c)
            send(src(3, core), dst(me, c), nb(dim, -1, core), S.take(), st["r"] + c)
        send(src(0, 1 - c), dst(me, c), {"row": 1 - c, "col": q}, S.take(), st["d"])
        return st

    def x_onward(p, dst, transit, st):
        dim = PARTS[p][2]
        me = pos[dim]
        return (make(transit.at[0], dst(rel(me, -1), c), nb(dim, 1, 0), st["f"][0], st["o"] + c),
                make(transit.at[1], dst(rel(me, 1), c), nb(dim, -1, 1), st["f"][1], st["o"] + c))

    def x_forward(p, dst, transit, st):
        for got, cp in zip(st["t"], x_onward(p, dst, transit, st)):
            got.wait_recv()
            cp.start()

    def x_wait(p, dst, transit, st):
        dim = PARTS[p][2]
        me = pos[dim]
        for core in range(2):
            wait_in(dst(rel(me, -1), core), st["l"] + core, nb(dim, -1, core))
            wait_in(dst(rel(me, 1), core), st["r"] + core, nb(dim, 1, core))
            wait_in(dst(rel(me, 2), core), st["o"] + core, nb(dim, 1, core))
        wait_in(dst(me, 1 - c), st["d"], {"row": 1 - c, "col": q})
        for cp in x_onward(p, dst, transit, st):
            cp.wait_send()

    def p_src(m, p):
        return lambda k, core: ag[p].at[m, :, :, pl.ds((2 * k + core) * CAP, CAP)]

    def p_dst(m, p):
        return lambda d3v, core: plane(recv[p].at[m], p, core, d3v)

    def r_src(m, p):
        return lambda k, core: plane(outp[p].at[m], p, core, rel(pos[PARTS[p][2]], k))

    def r_dst(m, p):
        return lambda d3v, core: r1[p].at[m, d3v, core]

    pst, loc = {}, {}

    def p_start(m, p):
        pst[m, p] = x_start(p, p_src(m, p), p_dst(m, p), ptr[p].at[m])
        cp = pltpu.make_async_copy(p_src(m, p)(0, c), p_dst(m, p)(pos[PARTS[p][2]], c), lsem.at[9 + m * 3 + p])
        cp.start()
        loc[m, p] = cp

    def p_forward(m, p):
        x_forward(p, p_dst(m, p), ptr[p].at[m], pst[m, p])

    def p_wait(m):
        for p in P3:
            x_wait(p, p_dst(m, p), ptr[p].at[m], pst[m, p])
            loc.pop((m, p)).wait()

    rows_t = RING * RING * CAP

    def tile_of(refs, m, i, p):
        return refs[p].at[m, i // 4, :, :, i % 4] if p == 2 else refs[p].at[m, i // 4, i % 4]

    def xload(m, i, slot):
        return [pltpu.make_async_copy(tile_of(recv, m, i, p), xbuf.at[slot, :, :, :, pl.ds(offs[p], COLS[p])],
                                      xsem.at[slot, p]) for p in P3]

    def ostore(m, i, slot):
        return [pltpu.make_async_copy(obuf.at[slot, :, :, :, pl.ds(offs[p], COLS[p])], tile_of(outp, m, i, p),
                                      osem.at[slot, p]) for p in P3]

    def expert(m, events):
        for cp in xload(m, 0, 0):
            cp.start()

        def tile(i, _):
            slot = i % 2

            @pl.when(i + 1 < TILES)
            def _():
                for cp in xload(m, i + 1, (i + 1) % 2):
                    cp.start()

            for at, todo in events.items():
                @pl.when(i == at)
                def _():
                    for f in todo:
                        f()

            for cp in xload(m, i, slot):
                cp.wait()

            @pl.when(i >= 2)
            def _():
                for cp in ostore(m, i - 2, slot):
                    cp.wait()

            xt = xbuf[slot].reshape(rows_t, D)
            h1 = jnp.dot(xt, w1[...], preferred_element_type=F32)
            h3 = jnp.dot(xt, w3[...], preferred_element_type=F32)
            act = (jax.nn.silu(h1) * h3).astype(BF)
            o = jnp.dot(act, w2[...], preferred_element_type=F32).astype(BF)
            obuf[slot] = o.reshape(RING, RING, CAP, D)
            for cp in ostore(m, i, slot):
                cp.start()
            return 0

        lax.fori_loop(0, TILES, tile, 0)
        for i in (TILES - 2, TILES - 1):
            for cp in ostore(m, i, i % 2):
                cp.wait()

    rst = {}

    def r1_load(m, p):
        return pltpu.make_async_copy(r_src(m, p)(0, c), lst[p], lsem.at[15 + p])

    def r1_store(m, p):
        return pltpu.make_async_copy(lst[p], r_dst(m, p)(pos[PARTS[p][2]], c), lsem.at[18 + p])

    def r1_start(m, p):
        if m == 1:
            r1_store(0, p).wait()
        rst[m, p] = x_start(p, r_src(m, p), r_dst(m, p), r1t[p].at[m])
        r1_load(m, p).start()

    def r1_forward(m, p):
        x_forward(p, r_dst(m, p), r1t[p].at[m], rst[m, p])
        r1_load(m, p).wait()
        r1_store(m, p).start()

    r2st = {}

    def r2_start(m, p):
        x_wait(p, r_dst(m, p), r1t[p].at[m], rst[m, p])
        if m == 1:
            r1_store(1, p).wait()
        dim = PARTS[p][1]
        me = pos[dim]
        src = r1[p].at[m]
        st = {}
        st["t"] = (send(src.at[pl.ds(0, 2), :, rel(me, 2)], r2t[p].at[m, 0], nb(dim, 1), S.take(), R.take()),
                   send(src.at[pl.ds(2, 2), :, rel(me, 2)], r2t[p].at[m, 1], nb(dim, -1), S.take(), R.take()))
        st["n"] = (send(src.at[:, :, rel(me, 1)], r2[p].at[m, me], nb(dim, 1), S.take(), R.take()),
                   send(src.at[:, :, rel(me, -1)], r2[p].at[m, me], nb(dim, -1), S.take(), R.take()))
        r2st[m, p] = st

    def r2_forward(m, p):
        dim = PARTS[p][1]
        me = pos[dim]
        st = r2st[m, p]
        st["t"][0].wait_recv()
        a = send(r2t[p].at[m, 0], r2[p].at[m, rel(me, -1), pl.ds(0, 2)], nb(dim, 1), S.take(), R.take())
        st["t"][1].wait_recv()
        b = send(r2t[p].at[m, 1], r2[p].at[m, rel(me, 1), pl.ds(2, 2)], nb(dim, -1), S.take(), R.take())
        st["f"] = (a, b)

    def r2_wait(m, p):
        st = r2st[m, p]
        for cp in st["n"] + st["f"]:
            cp.wait_recv()

    def stage_in(m, p, k, slot):
        d1, d2, d3 = PARTS[p]
        s1v = (pos[d1] + k) % RING
        cols = pl.ds(0, COLS[p])
        cps = [pltpu.make_async_copy(r1[p].at[m, :, :, pos[d2], s1v], stage.at[slot, 0, :, :, :, cols],
                                     csem.at[slot, 0])]
        for j in range(1, RING):
            cps.append(pltpu.make_async_copy(r2[p].at[m, rel(pos[d2], j), :, :, s1v], stage.at[slot, j, :, :, :, cols],
                                             csem.at[slot, j]))
        return cps

    def combine(m, p, lo, hi):
        n_e = 8 * RING
        slots = 2 * p
        k_of = lambda i: (2 - i + RING) % RING
        if lo == 0:
            for cp in stage_in(m, p, k_of(0), slots):
                cp.start()

        def one(i, _):
            k = k_of(i)
            slot = slots + i % 2

            @pl.when(i + 1 < RING)
            def _():
                for cp in stage_in(m, p, k_of(i + 1), slots + (i + 1) % 2):
                    cp.start()

            for cp in stage_in(m, p, k, slot):
                cp.wait()
            mask = spread(crank[p][m * 4 + k], n_e)
            rest_g = cgate[p][m * 4 + k]
            rows = stage[slot, :, :, :, :, 0:COLS[p]].reshape(n_e * CAP, COLS[p])
            acc = jnp.zeros((T, COLS[p]), F32)
            for _ in range(3):
                piece = rest_g.astype(BF).astype(F32)
                rest_g = rest_g - piece
                wt = jnp.where(mask, jnp.broadcast_to(piece[:, None, :], (n_e, CAP, T)), 0.0)
                wt = wt.reshape(n_e * CAP, T).astype(BF)
                acc = acc + lax.dot_general(wt, rows, (((0,), (0,)), ((), ())), preferred_element_type=F32)
            part_acc[p][m, k] = acc
            return 0

        lax.fori_loop(lo, hi, one, 0)

    r3 = {}

    def r3_one(m, p):
        dim = PARTS[p][0]
        half = T // 2
        a = send(part_acc[p].at[m, 2, pl.ds(0, half)], q1[p].at[m, 0], nb(dim, 1), S.take(), R.take())
        b = send(part_acc[p].at[m, 2, pl.ds(half, half)], q1[p].at[m, 1], nb(dim, -1), S.take(), R.take())
        r3[m, p] = [a, b]

    def r3_two(m, p):
        dim = PARTS[p][0]
        half = T // 2
        a, b = r3[m, p]
        a.wait_recv()
        part_acc[p][m, 1, 0:half] = part_acc[p][m, 1, 0:half] + q1[p][m, 0]
        a2 = send(part_acc[p].at[m, 1], q2[p].at[m, 0], nb(dim, 1), S.take(), R.take())
        b.wait_recv()
        part_acc[p][m, 3, half:T] = part_acc[p][m, 3, half:T] + q1[p][m, 1]
        b2 = send(part_acc[p].at[m, 3], q2[p].at[m, 1], nb(dim, -1), S.take(), R.take())
        r3[m, p] += [a2, b2]

    def r3_end(m, p):
        for cp in r3[m, p][2:]:
            cp.wait_recv()
        cols = slice(offs[p], offs[p] + COLS[p])
        acc = part_acc[p][m, 0] + q2[p][m, 0] + q2[p][m, 1]
        y_ref[m, :, cols] = (h_ref[m, :, cols].astype(F32) + acc).astype(BF)

    meta = {}

    def meta_one():
        meta["i"] = [ring1(PARTS[p][0], mi1(p)) for p in P3]
        meta["g"] = [ring1(PARTS[p][0], mg1(p)) for p in P3]

    def meta_two():
        meta["i"] = [ring2(PARTS[p][0], mi1(p), meta["i"][p]) for p in P3]
        meta["g"] = [ring2(PARTS[p][0], mg1(p), meta["g"][p]) for p in P3]

    def meta_three():
        for p in P3:
            ring3(meta["i"][p])
        meta["i"] = [ring1(PARTS[p][1], mi2(p)) for p in P3]

    def meta_four():
        meta["i"] = [ring2(PARTS[p][1], mi2(p), meta["i"][p]) for p in P3]

    def meta_five():
        for p in P3:
            ring3(meta["i"][p])
            ring3(meta["g"][p])
            tables(p)

    def slots_in(m, p):
        ring3(s1[m, p])
        build(m, p)

    def sums_one(m, p):
        r2_wait(m, p)
        combine(m, p, 0, 1)
        r3_one(m, p)

    def sums_two(m, p):
        combine(m, p, 1, RING)

    step = {"mt1": meta_one, "mt2": meta_two, "mt3": meta_three, "mt4": meta_four, "tab": meta_five,
            "a1": a_one, "a2": a_two, "a3": a_three, "a4": a_four, "bd": slots_in, "ps": p_start, "pf": p_forward,
            "q1": r1_start, "qf": r1_forward, "q2": r2_start, "qg": r2_forward,
            "ca": sums_one, "cb": sums_two, "r3": r3_two, "fin": r3_end}

    def do(name):
        head, _, tail = name.partition("_")
        step[head](*(int(v) for v in tail))

    queue = list(ORDER)
    while queue:
        name = queue.pop(0)
        if name[0] != "E":
            do(name)
            continue
        m = int(name[1])
        events, at = {}, 1
        while at < TILES:
            nxt = queue.pop(0)
            if nxt[0] == "E":
                at += 1
            else:
                events.setdefault(at, []).append(functools.partial(do, nxt))
        if m == 0:
            for cp in wload:
                cp.wait()
        p_wait(m)
        expert(m, events)
    for cp in list(pending.values()):
        cp.wait_send()
    if S.n > nsem or R.n > nsem:
        raise ValueError(f"{S.n} {R.n}")


NSEM = 252


def moe(z, h, idx, gates, w1, w3, w2, cap):
    _, T, D = z.shape
    FF = w1.shape[-1]
    TOP = idx.shape[1]
    COLS = widths(D)
    dims = (T, D, FF, cap, TOP, COLS)
    hbm = []
    for lead in ((2, 2, 4, 4, 4), (2, 2, 4, 4, 4), (2, 2, 4, 4), (2, 4, 2, 4, 4), (2, 2, 4, 4),
                 (2, 4, 4, 2, 4), (2, 2, 2, 2, 4)):
        for p in range(3):
            hbm.append(jax.ShapeDtypeStruct(lead + (cap, COLS[p]), BF))
    V = pltpu.VMEM
    scratch = [V((2, 4, 4, T, COLS[p]), BF) for p in range(3)]
    scratch += [V((3, 4, 4, 2, TOP, T), jnp.int32), V((3, 4, 2, TOP, T), F32)]
    scratch += [V((4, 4, cap, COLS[p]), BF) for p in range(3)]
    scratch += [V((D, FF), BF), V((D, FF), BF), V((FF, D), BF), V((2, 4, 4, cap, D), BF), V((2, 4, 4, cap, D), BF)]
    scratch += [V((6, 4, 4, 2, cap, max(COLS)), BF)]
    scratch += [V((2, 4, T, COLS[p]), F32) for p in range(3)]
    scratch += [V((2, 2, T // 2, COLS[p]), F32) for p in range(3)]
    scratch += [V((2, 2, T, COLS[p]), F32) for p in range(3)]
    scratch += [V((32, 8, T), F32)] * 3 + [V((8, 32, T), F32)] * 6
    DMA = pltpu.SemaphoreType.DMA
    scratch += [DMA((NSEM,)), DMA((NSEM,)), DMA((2, 3)), DMA((2, 3)), DMA((21,)), DMA((6, 4))]
    any_spec = pl.BlockSpec(memory_space=pl.ANY)
    vm = pl.BlockSpec(memory_space=pltpu.VMEM)
    out = pl.pallas_call(
        functools.partial(moe_kernel, dims, NSEM),
        out_shape=[jax.ShapeDtypeStruct((2, T, D), BF)] + hbm,
        in_specs=[any_spec, vm, vm, vm, any_spec, any_spec, any_spec],
        out_specs=[vm] + [any_spec] * len(hbm),
        scratch_shapes=scratch,
        compiler_params=pltpu.CompilerParams(collective_id=0, has_side_effects=True, vmem_limit_bytes=VMEM_LIMIT),
    )(z, h, idx, gates, w1, w3, w2)
    return out[0]


def attn_kernel(nb, heads, groups, x_ref, ga_ref, gm_ref, wq_ref, wk_ref, wv_ref, wo_ref, h_ref, z_ref,
                u_ref, q_ref, k_ref, v_ref, acc_ref):
    i = pl.program_id(0)
    seq = x_ref.shape[1]
    d = x_ref.shape[2]

    def norm(v, g):
        return (v * lax.rsqrt(jnp.mean(v * v, axis=-1, keepdims=True) + 1e-6) * g).astype(BF)

    @pl.when(i == 0)
    def _():
        u_ref[...] = norm(x_ref[...].reshape(nb * seq, d).astype(F32), ga_ref[...])
        acc_ref[...] = jnp.zeros_like(acc_ref)
        q_ref[...] = jnp.zeros_like(q_ref)
        k_ref[...] = jnp.zeros_like(k_ref)
        v_ref[...] = jnp.zeros_like(v_ref)

    q, k, v = q_ref[...], k_ref[...], v_ref[...]
    causal = (lax.broadcasted_iota(jnp.int32, (seq, seq), 0) >= lax.broadcasted_iota(jnp.int32, (seq, seq), 1))
    u = u_ref[...]
    qn = jnp.dot(u, wq_ref[...], preferred_element_type=F32).astype(BF)
    kn = jnp.dot(u, wk_ref[...], preferred_element_type=F32).astype(BF)
    vn = jnp.dot(u, wv_ref[...], preferred_element_type=F32).astype(BF)
    rows = []
    for b in range(nb):
        cols = []
        for hd in range(heads):
            r, e = slice(b * seq, (b + 1) * seq), slice(hd * HEAD, (hd + 1) * HEAD)
            s = lax.dot_general(q[r, e], k[r, e], (((1,), (1,)), ((), ())), preferred_element_type=F32) * HEAD ** -0.5
            s = jnp.where(causal, s, -1e30)
            p = jnp.exp(s - jnp.max(s, axis=-1, keepdims=True))
            p = (p / jnp.sum(p, axis=-1, keepdims=True)).astype(BF)
            cols.append(jnp.dot(p, v[r, e], preferred_element_type=F32).astype(BF))
        rows.append(jnp.concatenate(cols, axis=1))
    o = jnp.concatenate(rows, axis=0)
    acc_ref[...] += jnp.dot(o, wo_ref[...], preferred_element_type=F32)
    q_ref[...], k_ref[...], v_ref[...] = qn, kn, vn

    @pl.when(i == groups)
    def _():
        h = (x_ref[...].reshape(nb * seq, d).astype(F32) + acc_ref[...]).astype(BF)
        h_ref[...] = h.reshape(nb, seq, d)
        z_ref[...] = norm(h.astype(F32), gm_ref[...]).reshape(nb, seq, d)


def attention(x, wq, wk, wv, wo, gattn, gmoe):
    nb, seq, d = x.shape
    width = wq.shape[1]
    heads = HEADS_PER_STEP
    cols = heads * HEAD
    groups = width // cols
    now = lambda i: jnp.minimum(i, groups - 1)
    whole = pl.BlockSpec((nb, seq, d), lambda i: (0, 0, 0))
    gain = pl.BlockSpec((1, d), lambda i: (0, 0))
    proj = pl.BlockSpec((d, cols), lambda i: (0, now(i)))
    V = pltpu.VMEM
    return pl.pallas_call(
        functools.partial(attn_kernel, nb, heads, groups),
        grid=(groups + 1,),
        out_shape=[jax.ShapeDtypeStruct((nb, seq, d), BF)] * 2,
        in_specs=[whole, gain, gain, proj, proj, proj,
                  pl.BlockSpec((cols, d), lambda i: (jnp.maximum(i - 1, 0), 0))],
        out_specs=[whole, whole],
        scratch_shapes=[V((nb * seq, d), BF)] + [V((nb * seq, cols), BF)] * 3 + [V((nb * seq, d), F32)],
        compiler_params=pltpu.CompilerParams(dimension_semantics=("arbitrary",), vmem_limit_bytes=VMEM_LIMIT),
    )(x, gattn.reshape(1, d), gmoe.reshape(1, d), wq, wk, wv, wo)


def capacity(t, top, n_exp):
    return ((top * ((2 * t + n_exp - 1) // n_exp) + 7) // 8) * 8


def solution(mesh):
    ep_axes = ("row", "col")
    tok_axes = ("dp", "row", "col")
    ep = mesh.shape["row"] * mesh.shape["col"]

    def local(x, idx, gates, wq, wk, wv, wo, gattn, gmoe, w1, w3, w2):
        seq, d = x.shape[2:]
        top = idx.shape[-1]
        cap = capacity(seq, top, ep)
        h, z = attention(x[:, 0], wq, wk, wv, wo, gattn, gmoe)
        y = moe(z, h, jnp.swapaxes(idx[:, 0], 1, 2), jnp.swapaxes(gates[:, 0], 1, 2), w1, w3, w2, cap)
        return y[:, None]

    tok_spec = P(None, tok_axes)
    exp_spec = P(ep_axes)
    return jax.shard_map(local, mesh=mesh,
                         in_specs=(tok_spec, tok_spec, tok_spec, P(), P(), P(), P(), P(), P(), exp_spec, exp_spec, exp_spec),
                         out_specs=tok_spec, check_vma=False)
```

time: 372 us -> 338 us (0.909)
  the two profiles are of different devices: /device:TPU:10 before, /device:TPU:0 now
where the time goes in v2:
time: 338 us
  Pallas kernels  335 us (99%)
    pallas_call x1, Pallas kernels, moe(): pl.pallas_call(functools.partial(moe_kernel, dims, NSEM), out_shape=[jax....  287 us
    pallas_call x1, Pallas kernels, attention(): pl.pallas_call(functools.partial(attn_kernel, nb, heads, groups), grid=(g...  49 us

profile of v2, /device:TPU:0, one launch (start us, length us, event | category | flops | bytes accessed | tf_op | source)
XLA Modules:
  0.0 337.8 jit_solution(2564088366371780267)
XLA Ops:
  0.0 49.0 %shard_map.118 = (bf16[2,128,2048]{2,1,0:T(8,128)(2,1)}, bf16[2,128,2048]{2,1,0:T(8,128)(2,1)}) custom-call(bf16[2,128,2048]{2,1,0:T(8,128)(2,1)} %bitcast.12, f32[1,2048]{1,0:T(1,128)} %bitcast.14, f32[1,2048]{1,0:T(1,128)} %bitcast.15, bf16[2048,4096]{1,0:T(8,128)(2,1)} %wq_ref.1, bf16[2048,4096]{1,0:T(8,128)(2,1)} %wk_ref.1, bf16[2048,4096]{1,0:T(8,128)(2,1)} %wv_ref.1, ...), custom_call_target="tpu_custom_call" | custom-call | tf_op jit(solution)/shard_map/pallas_call | solution.py:676
  49.0 286.5 %shard_map.119 = (bf16[2,128,2048]{2,1,0:T(8,128)(2,1)}, bf16[2,2,4,4,4,16,640]{6,5,4,3,2,1,0:T(8,128)(2,1)}, bf16[2,2,4,4,4,16,640]{6,5,4,3,2,1,0:T(8,128)(2,1)...) custom-call(bf16[2,128,2048]{2,1,0:T(8,128)(2,1)} %get-tuple-element, ...), custom_call_target="tpu_custom_call" | custom-call | tf_op jit(solution)/shard_map/pallas_call | solution.py:609
  335.5 2.3 copy.15

commit v3 on v2

--- a/solution.py
+++ b/solution.py
@@ -9,17 +9,17 @@
 
 HEAD = 128
 VMEM_LIMIT = 67_000_000
-HEADS_PER_STEP = 2
+HEADS_PER_STEP = 4
 ORDER = (
-    "mt1", "a1_02", "a1_00", "a1_01", "mt2", "a1_11", "a1_10", "a2_00", "a2_02", "mt3", "a2_10", "a2_01", "a2_11",
-    "mt4", "a1_12", "a3_02", "a3_00", "a3_11", "a2_12", "a3_10", "a3_01", "tab", "a4_02", "a4_00", "a3_12", "bd_02",
-    "a4_01", "a4_10", "ps_02", "a4_11", "bd_00", "a4_12", "bd_01", "ps_00", "ps_01", "bd_11", "pf_02", "pf_01",
-    "bd_10", "ps_11", "pf_00", "bd_12", "ps_12", "ps_10", "E0_0", "E0_1", "pf_10", "E0_2", "pf_11", "E0_3", "E0_4",
-    "pf_12", "E0_5", "E0_6", "E0_7", "q1_01", "q1_02", "q1_00", "E1_0", "E1_1", "E1_2", "E1_3", "qf_01", "E1_4",
-    "E1_5", "qf_02", "qf_00", "E1_6", "E1_7", "q1_11", "q1_10", "q1_12", "q2_02", "qf_10", "qf_11", "q2_01", "qf_12",
-    "q2_10", "qg_10", "qg_02", "q2_12", "qg_01", "q2_11", "ca_02", "q2_00", "qg_00", "qg_12", "ca_10", "qg_11",
-    "cb_02", "cb_10", "r3_02", "ca_01", "cb_01", "ca_11", "cb_11", "ca_12", "ca_00", "r3_01", "r3_10", "cb_12",
-    "fin_02", "r3_12", "cb_00", "r3_00", "r3_11", "fin_10", "fin_01", "fin_12", "fin_11", "fin_00",
+    "mt1", "a1_00", "a1_01", "a1_10", "a1_11", "a1_02", "mt2", "a2_02", "a2_00", "a2_01", "a1_12", "mt3", "a3_02",
+    "a3_00", "a3_01", "a2_10", "mt4", "a2_11", "a2_12", "a4_00", "a4_02", "a3_11", "a3_12", "a4_01", "a3_10", "tab",
+    "bd_00", "bd_02", "ps_00", "ps_02", "a4_11", "a4_12", "bd_01", "a4_10", "ps_01", "pf_02", "pf_00", "bd_12",
+    "bd_11", "pf_01", "ps_11", "bd_10", "ps_10", "ps_12", "E0_0", "E0_1", "E0_2", "E0_3", "pf_11", "pf_10", "E0_4",
+    "pf_12", "E0_5", "E0_6", "E0_7", "q1_01", "q1_02", "q1_00", "E1_0", "E1_1", "E1_2", "E1_3", "E1_4", "qf_00",
+    "qf_01", "qf_02", "E1_5", "E1_6", "E1_7", "q1_11", "q1_12", "q1_10", "q2_02", "qf_10", "q2_01", "qf_12", "q2_10",
+    "qf_11", "qg_01", "qg_02", "q2_12", "qg_10", "q2_11", "ca_02", "q2_00", "cb_02", "qg_00", "ca_01", "qg_12",
+    "qg_11", "ca_10", "r3_02", "cb_01", "cb_10", "ca_11", "cb_11", "ca_12", "ca_00", "r3_01", "r3_10", "cb_12",
+    "r3_12", "cb_00", "r3_11", "r3_00", "fin_02", "fin_10", "fin_01", "fin_12", "fin_11", "fin_00",
 )
 
 
@@ -28,6 +28,7 @@
 F32 = jnp.float32
 RING = 4
 CORES = 2
+MICRO = 2
 COEF = {"z": 16, "y": 4, "x": 1}
 PARTS = (("x", "y", "z"), ("y", "z", "x"), ("z", "x", "y"))
 TILES = CORES * RING
@@ -78,7 +79,7 @@
     q = lax.axis_index("col")
     pos = {"z": q // 16, "y": (q // 4) % 4, "x": q % 4}
     S, R = Sems(), Sems()
-    pending = {}
+    unsent = []
     offs = (0, COLS[0], COLS[0] + COLS[1])
 
     def rel(v, s):
@@ -94,14 +95,13 @@
                                             device_id=dev, device_id_type=MESH)
 
     def send(src, dst, dev, si, ri):
-        cp = make(src, dst, dev, si, ri)
-        cp.start()
-        pending[id(cp)] = cp
-        return cp
-
-    def wait_in(ref, ri, dev):
-        pltpu.make_async_remote_copy(src_ref=ref, dst_ref=ref, send_sem=ssem.at[0], recv_sem=rsem.at[ri],
-                                     device_id=dev, device_id_type=MESH).wait_recv()
+        make(src, dst, dev, si, ri).start()
+
+    def wait_in(ref, ri):
+        make(ref, ref, nb("x", 1), 0, ri).wait_recv()
+
+    def wait_out(ref, si):
+        make(ref, ref, nb("x", 1), si, 0).wait_send()
 
     barrier = pltpu.get_barrier_semaphore()
     friends = [nb(d, s, core) for d in "xyz" for s in (1, -1) for core in (c, 1 - c)]
@@ -127,21 +127,20 @@
 
     def ring1(dim, block):
         me = pos[dim]
-        a = send(block(me, None), block(me, None), nb(dim, 1), S.take(), R.take())
-        b = send(block(me, None), block(me, None), nb(dim, -1), S.take(), R.take())
-        return a, b
-
-    def ring2(dim, block, ab):
-        me = pos[dim]
-        ab[0].wait_recv()
-        a = send(block(rel(me, -1), 0), block(rel(me, -1), 0), nb(dim, 1), S.take(), R.take())
-        ab[1].wait_recv()
-        b = send(block(rel(me, 1), 1), block(rel(me, 1), 1), nb(dim, -1), S.take(), R.take())
-        return a, b
-
-    def ring3(ab):
-        ab[0].wait_recv()
-        ab[1].wait_recv()
+        g = (S.take(), R.take(), R.take(), R.take())
+        send(block(me, None), block(me, None), nb(dim, 1), g[0], g[1])
+        send(block(me, None), block(me, None), nb(dim, -1), g[0], g[2])
+        return g
+
+    def ring2(dim, block, g):
+        left, right = rel(pos[dim], -1), rel(pos[dim], 1)
+        wait_in(block(left, None), g[1])
+        send(block(left, 0), block(left, 0), nb(dim, 1), g[0], g[3])
+        wait_in(block(right, None), g[2])
+        send(block(right, 1), block(right, 1), nb(dim, -1), g[0], g[3])
+
+    def ring3(dim, block, g):
+        wait_in(block(rel(pos[dim], 2), None), g[3])
 
     def blk1(m, p):
         d2 = PARTS[p][1]
@@ -183,25 +182,26 @@
         return f
 
     P3 = range(3)
-    s1, asends = {}, {}
+    g1, g2 = {}, {}
 
     def a_one(m, p):
         own[m, p].wait()
-        s1[m, p] = ring1(PARTS[p][0], blk1(m, p))
-        asends[m, p] = list(s1[m, p])
+        g1[m, p] = ring1(PARTS[p][0], blk1(m, p))
 
     def a_two(m, p):
-        s1[m, p] = ring2(PARTS[p][0], blk1(m, p), s1[m, p])
-        asends[m, p] += s1[m, p]
+        ring2(PARTS[p][0], blk1(m, p), g1[m, p])
 
     def a_three(m, p):
-        ring3(s1[m, p])
-        s1[m, p] = ring1(PARTS[p][1], blk2(m, p))
-        asends[m, p] += s1[m, p]
+        ring3(PARTS[p][0], blk1(m, p), g1[m, p])
+        g2[m, p] = ring1(PARTS[p][1], blk2(m, p))
 
     def a_four(m, p):
-        s1[m, p] = ring2(PARTS[p][1], blk2(m, p), s1[m, p])
-        asends[m, p] += s1[m, p]
+        ring2(PARTS[p][1], blk2(m, p), g2[m, p])
+
+    def a_done(m, p):
+        ring3(PARTS[p][1], blk2(m, p), g2[m, p])
+        wait_out(ag[p].at[m, pos[PARTS[p][1]], pl.ds(0, 3)], g1[m, p][0])
+        wait_out(ag[p].at[m, pl.ds(0, 3)], g2[m, p][0])
 
     before = (lax.broadcasted_iota(jnp.int32, (T, T), 0) < lax.broadcasted_iota(jnp.int32, (T, T), 1)).astype(BF)
 
@@ -233,7 +233,7 @@
             return 0
 
         lax.fori_loop(0, 32, one, 0)
-        drank[p][...] = ranks(drank[p][...].reshape(32 * 8, T)).reshape(32, 8, T)
+        drank[p][...] = ranks(drank[p][...].reshape(-1, T)).reshape(drank[p].shape)
         n_e = 8 * RING
         r = lax.broadcasted_iota(jnp.int32, (n_e, T), 0)
         e = (r % 2) * 64 + COEF[d3] * ((r // 2) % RING) + COEF[d2] * ((pos[d2] + r // 8) % RING) + COEF[d1] * pos[d1]
@@ -248,10 +248,6 @@
         lax.fori_loop(0, 8, two, 0)
 
     def build(m, p):
-        for cp in asends.pop((m, p)):
-            cp.wait_send()
-            del pending[id(cp)]
-
         def one(s, _):
             sel = jnp.where(spread(drank[p][m * 16 + s], 8), 1.0, 0.0).reshape(8 * CAP, T).astype(BF)
             rows = jnp.dot(sel, ag[p][m, s // 4, s % 4], preferred_element_type=F32)
@@ -270,38 +266,27 @@
     def x_start(p, src, dst, transit):
         dim = PARTS[p][2]
         me = pos[dim]
-        st = {}
-        st["t"] = (send(src(2, 0), transit.at[0], nb(dim, 1), S.take(), R.take()),
-                   send(src(2, 1), transit.at[1], nb(dim, -1), S.take(), R.take()))
-        st["l"], st["r"], st["o"], st["d"] = R.take(2), R.take(2), R.take(2), R.take()
-        st["f"] = (S.take(), S.take())
+        st = {"s": S.take(), "d": S.take(), "r": R.take(), "t": (R.take(), R.take())}
+        send(src(2, 0), transit.at[0], nb(dim, 1), st["s"], st["t"][0])
+        send(src(2, 1), transit.at[1], nb(dim, -1), st["s"], st["t"][1])
         for core in range(2):
-            send(src(1, core), dst(me, c), nb(dim, 1, core), S.take(), st["l"] + c)
-            send(src(3, core), dst(me, c), nb(dim, -1, core), S.take(), st["r"] + c)
-        send(src(0, 1 - c), dst(me, c), {"row": 1 - c, "col": q}, S.take(), st["d"])
+            send(src(1, core), dst(me, c), nb(dim, 1, core), st["s"], st["r"])
+            send(src(3, core), dst(me, c), nb(dim, -1, core), st["s"], st["r"])
+        send(src(0, 1 - c), dst(me, c), {"row": 1 - c, "col": q}, st["d"], st["r"])
         return st
 
-    def x_onward(p, dst, transit, st):
+    def x_forward(p, dst, transit, st):
         dim = PARTS[p][2]
         me = pos[dim]
-        return (make(transit.at[0], dst(rel(me, -1), c), nb(dim, 1, 0), st["f"][0], st["o"] + c),
-                make(transit.at[1], dst(rel(me, 1), c), nb(dim, -1, 1), st["f"][1], st["o"] + c))
-
-    def x_forward(p, dst, transit, st):
-        for got, cp in zip(st["t"], x_onward(p, dst, transit, st)):
-            got.wait_recv()
-            cp.start()
-
-    def x_wait(p, dst, transit, st):
-        dim = PARTS[p][2]
-        me = pos[dim]
-        for core in range(2):
-            wait_in(dst(rel(me, -1), core), st["l"] + core, nb(dim, -1, core))
-            wait_in(dst(rel(me, 1), core), st["r"] + core, nb(dim, 1, core))
-            wait_in(dst(rel(me, 2), core), st["o"] + core, nb(dim, 1, core))
-        wait_in(dst(me, 1 - c), st["d"], {"row": 1 - c, "col": q})
-        for cp in x_onward(p, dst, transit, st):
-            cp.wait_send()
+        wait_in(transit.at[0], st["t"][0])
+        send(transit.at[0], dst(rel(me, -1), c), nb(dim, 1, 0), st["s"], st["r"])
+        wait_in(transit.at[1], st["t"][1])
+        send(transit.at[1], dst(rel(me, 1), c), nb(dim, -1, 1), st["s"], st["r"])
+
+    def x_wait(p, whole, dst, st):
+        wait_in(whole, st["r"])
+        unsent.append((whole, st["s"]))
+        unsent.append((dst(pos[PARTS[p][2]], c), st["d"]))
 
     def p_src(m, p):
         return lambda k, core: ag[p].at[m, :, :, pl.ds((2 * k + core) * CAP, CAP)]
@@ -315,21 +300,18 @@
     def r_dst(m, p):
         return lambda d3v, core: r1[p].at[m, d3v, core]
 
-    pst, loc = {}, {}
+    pst = {}
 
     def p_start(m, p):
         pst[m, p] = x_start(p, p_src(m, p), p_dst(m, p), ptr[p].at[m])
-        cp = pltpu.make_async_copy(p_src(m, p)(0, c), p_dst(m, p)(pos[PARTS[p][2]], c), lsem.at[9 + m * 3 + p])
-        cp.start()
-        loc[m, p] = cp
+        pltpu.make_async_copy(p_src(m, p)(0, c), p_dst(m, p)(pos[PARTS[p][2]], c), rsem.at[pst[m, p]["r"]]).start()
 
     def p_forward(m, p):
         x_forward(p, p_dst(m, p), ptr[p].at[m], pst[m, p])
 
     def p_wait(m):
         for p in P3:
-            x_wait(p, p_dst(m, p), ptr[p].at[m], pst[m, p])
-            loc.pop((m, p)).wait()
+            x_wait(p, recv[p].at[m], p_dst(m, p), pst[m, p])
 
     rows_t = RING * RING * CAP
 
@@ -388,14 +370,12 @@
     rst = {}
 
     def r1_load(m, p):
-        return pltpu.make_async_copy(r_src(m, p)(0, c), lst[p], lsem.at[15 + p])
+        return pltpu.make_async_copy(r_src(m, p)(0, c), lst[p].at[m], lsem.at[9 + m * 3 + p])
 
     def r1_store(m, p):
-        return pltpu.make_async_copy(lst[p], r_dst(m, p)(pos[PARTS[p][2]], c), lsem.at[18 + p])
+        return pltpu.make_async_copy(lst[p].at[m], r_dst(m, p)(pos[PARTS[p][2]], c), rsem.at[rst[m, p]["r"]])
 
     def r1_start(m, p):
-        if m == 1:
-            r1_store(0, p).wait()
         rst[m, p] = x_start(p, r_src(m, p), r_dst(m, p), r1t[p].at[m])
         r1_load(m, p).start()
 
@@ -407,33 +387,30 @@
     r2st = {}
 
     def r2_start(m, p):
-        x_wait(p, r_dst(m, p), r1t[p].at[m], rst[m, p])
-        if m == 1:
-            r1_store(1, p).wait()
+        x_wait(p, r1[p].at[m], r_dst(m, p), rst[m, p])
         dim = PARTS[p][1]
         me = pos[dim]
         src = r1[p].at[m]
-        st = {}
-        st["t"] = (send(src.at[pl.ds(0, 2), :, rel(me, 2)], r2t[p].at[m, 0], nb(dim, 1), S.take(), R.take()),
-                   send(src.at[pl.ds(2, 2), :, rel(me, 2)], r2t[p].at[m, 1], nb(dim, -1), S.take(), R.take()))
-        st["n"] = (send(src.at[:, :, rel(me, 1)], r2[p].at[m, me], nb(dim, 1), S.take(), R.take()),
-                   send(src.at[:, :, rel(me, -1)], r2[p].at[m, me], nb(dim, -1), S.take(), R.take()))
+        st = {"s": S.take(), "r": R.take(), "t": (R.take(), R.take())}
+        send(src.at[pl.ds(0, 2), :, rel(me, 2)], r2t[p].at[m, 0], nb(dim, 1), st["s"], st["t"][0])
+        send(src.at[pl.ds(2, 2), :, rel(me, 2)], r2t[p].at[m, 1], nb(dim, -1), st["s"], st["t"][1])
+        send(src.at[:, :, rel(me, 1)], r2[p].at[m, me], nb(dim, 1), st["s"], st["r"])
+        send(src.at[:, :, rel(me, -1)], r2[p].at[m, me], nb(dim, -1), st["s"], st["r"])
         r2st[m, p] = st
 
     def r2_forward(m, p):
         dim = PARTS[p][1]
         me = pos[dim]
         st = r2st[m, p]
-        st["t"][0].wait_recv()
-        a = send(r2t[p].at[m, 0], r2[p].at[m, rel(me, -1), pl.ds(0, 2)], nb(dim, 1), S.take(), R.take())
-        st["t"][1].wait_recv()
-        b = send(r2t[p].at[m, 1], r2[p].at[m, rel(me, 1), pl.ds(2, 2)], nb(dim, -1), S.take(), R.take())
-        st["f"] = (a, b)
+        wait_in(r2t[p].at[m, 0], st["t"][0])
+        send(r2t[p].at[m, 0], r2[p].at[m, rel(me, -1), pl.ds(0, 2)], nb(dim, 1), st["s"], st["r"])
+        wait_in(r2t[p].at[m, 1], st["t"][1])
+        send(r2t[p].at[m, 1], r2[p].at[m, rel(me, 1), pl.ds(2, 2)], nb(dim, -1), st["s"], st["r"])
 
     def r2_wait(m, p):
         st = r2st[m, p]
-        for cp in st["n"] + st["f"]:
-            cp.wait_recv()
+        wait_in(r2[p].at[m, pl.ds(0, 3)], st["r"])
+        unsent.append((r2[p].at[m], st["s"]))
 
     def stage_in(m, p, k, slot):
         d1, d2, d3 = PARTS[p]
@@ -485,25 +462,25 @@
     def r3_one(m, p):
         dim = PARTS[p][0]
         half = T // 2
-        a = send(part_acc[p].at[m, 2, pl.ds(0, half)], q1[p].at[m, 0], nb(dim, 1), S.take(), R.take())
-        b = send(part_acc[p].at[m, 2, pl.ds(half, half)], q1[p].at[m, 1], nb(dim, -1), S.take(), R.take())
-        r3[m, p] = [a, b]
+        st = {"s": S.take(), "r": R.take(), "t": (R.take(), R.take())}
+        send(part_acc[p].at[m, 2, pl.ds(0, half)], q1[p].at[m, 0], nb(dim, 1), st["s"], st["t"][0])
+        send(part_acc[p].at[m, 2, pl.ds(half, half)], q1[p].at[m, 1], nb(dim, -1), st["s"], st["t"][1])
+        r3[m, p] = st
 
     def r3_two(m, p):
         dim = PARTS[p][0]
         half = T // 2
-        a, b = r3[m, p]
-        a.wait_recv()
+        st = r3[m, p]
+        wait_in(q1[p].at[m, 0], st["t"][0])
         part_acc[p][m, 1, 0:half] = part_acc[p][m, 1, 0:half] + q1[p][m, 0]
-        a2 = send(part_acc[p].at[m, 1], q2[p].at[m, 0], nb(dim, 1), S.take(), R.take())
-        b.wait_recv()
+        send(part_acc[p].at[m, 1], q2[p].at[m, 0], nb(dim, 1), st["s"], st["r"])
+        wait_in(q1[p].at[m, 1], st["t"][1])
         part_acc[p][m, 3, half:T] = part_acc[p][m, 3, half:T] + q1[p][m, 1]
-        b2 = send(part_acc[p].at[m, 3], q2[p].at[m, 1], nb(dim, -1), S.take(), R.take())
-        r3[m, p] += [a2, b2]
+        send(part_acc[p].at[m, 3], q2[p].at[m, 1], nb(dim, -1), st["s"], st["r"])
 
     def r3_end(m, p):
-        for cp in r3[m, p][2:]:
-            cp.wait_recv()
+        wait_in(q2[p].at[m], r3[m, p]["r"])
+        unsent.append((part_acc[p].at[m, pl.ds(0, 3)], r3[m, p]["s"]))
         cols = slice(offs[p], offs[p] + COLS[p])
         acc = part_acc[p][m, 0] + q2[p][m, 0] + q2[p][m, 1]
         y_ref[m, :, cols] = (h_ref[m, :, cols].astype(F32) + acc).astype(BF)
@@ -511,29 +488,34 @@
     meta = {}
 
     def meta_one():
-        meta["i"] = [ring1(PARTS[p][0], mi1(p)) for p in P3]
-        meta["g"] = [ring1(PARTS[p][0], mg1(p)) for p in P3]
+        for p in P3:
+            meta[p] = [ring1(PARTS[p][0], mi1(p)), ring1(PARTS[p][0], mg1(p))]
 
     def meta_two():
-        meta["i"] = [ring2(PARTS[p][0], mi1(p), meta["i"][p]) for p in P3]
-        meta["g"] = [ring2(PARTS[p][0], mg1(p), meta["g"][p]) for p in P3]
+        for p in P3:
+            ring2(PARTS[p][0], mi1(p), meta[p][0])
+            ring2(PARTS[p][0], mg1(p), meta[p][1])
 
     def meta_three():
         for p in P3:
-            ring3(meta["i"][p])
-        meta["i"] = [ring1(PARTS[p][1], mi2(p)) for p in P3]
+            ring3(PARTS[p][0], mi1(p), meta[p][0])
+            meta[p].append(ring1(PARTS[p][1], mi2(p)))
 
     def meta_four():
-        meta["i"] = [ring2(PARTS[p][1], mi2(p), meta["i"][p]) for p in P3]
+        for p in P3:
+            ring2(PARTS[p][1], mi2(p), meta[p][2])
 
     def meta_five():
         for p in P3:
-            ring3(meta["i"][p])
-            ring3(meta["g"][p])
+            ring3(PARTS[p][1], mi2(p), meta[p][2])
+            ring3(PARTS[p][0], mg1(p), meta[p][1])
             tables(p)
+            unsent.append((mi.at[p, pos[PARTS[p][1]], pl.ds(0, 3)], meta[p][0][0]))
+            unsent.append((mg.at[p, pl.ds(0, 3)], meta[p][1][0]))
+            unsent.append((mi.at[p, pl.ds(0, 3)], meta[p][2][0]))
 
     def slots_in(m, p):
-        ring3(s1[m, p])
+        a_done(m, p)
         build(m, p)
 
     def sums_one(m, p):
@@ -572,13 +554,13 @@
                 cp.wait()
         p_wait(m)
         expert(m, events)
-    for cp in list(pending.values()):
-        cp.wait_send()
-    if S.n > nsem or R.n > nsem:
+    for ref, si in unsent:
+        wait_out(ref, si)
+    if (S.n, R.n) != nsem:
         raise ValueError(f"{S.n} {R.n}")
 
 
-NSEM = 252
+NSEM = (57, 135)
 
 
 def moe(z, h, idx, gates, w1, w3, w2, cap):
@@ -588,22 +570,24 @@
     COLS = widths(D)
     dims = (T, D, FF, cap, TOP, COLS)
     hbm = []
-    for lead in ((2, 2, 4, 4, 4), (2, 2, 4, 4, 4), (2, 2, 4, 4), (2, 4, 2, 4, 4), (2, 2, 4, 4),
-                 (2, 4, 4, 2, 4), (2, 2, 2, 2, 4)):
-        for p in range(3):
+    B, C, R, H, P3 = MICRO, CORES, RING, RING // 2, range(3)
+    for lead in ((B, C, R, R, R), (B, C, R, R, R), (B, C, R, R), (B, R, C, R, R), (B, C, R, R),
+                 (B, R, R, C, R), (B, C, H, C, R)):
+        for p in P3:
             hbm.append(jax.ShapeDtypeStruct(lead + (cap, COLS[p]), BF))
     V = pltpu.VMEM
-    scratch = [V((2, 4, 4, T, COLS[p]), BF) for p in range(3)]
-    scratch += [V((3, 4, 4, 2, TOP, T), jnp.int32), V((3, 4, 2, TOP, T), F32)]
-    scratch += [V((4, 4, cap, COLS[p]), BF) for p in range(3)]
-    scratch += [V((D, FF), BF), V((D, FF), BF), V((FF, D), BF), V((2, 4, 4, cap, D), BF), V((2, 4, 4, cap, D), BF)]
-    scratch += [V((6, 4, 4, 2, cap, max(COLS)), BF)]
-    scratch += [V((2, 4, T, COLS[p]), F32) for p in range(3)]
-    scratch += [V((2, 2, T // 2, COLS[p]), F32) for p in range(3)]
-    scratch += [V((2, 2, T, COLS[p]), F32) for p in range(3)]
-    scratch += [V((32, 8, T), F32)] * 3 + [V((8, 32, T), F32)] * 6
+    scratch = [V((B, R, R, T, COLS[p]), BF) for p in P3]
+    scratch += [V((3, R, R, B, TOP, T), jnp.int32), V((3, R, B, TOP, T), F32)]
+    scratch += [V((B, R, R, cap, COLS[p]), BF) for p in P3]
+    scratch += [V((D, FF), BF), V((D, FF), BF), V((FF, D), BF), V((C, R, R, cap, D), BF), V((C, R, R, cap, D), BF)]
+    scratch += [V((3 * C, R, R, C, cap, max(COLS)), BF)]
+    scratch += [V((B, R, T, COLS[p]), F32) for p in P3]
+    scratch += [V((B, C, T // 2, COLS[p]), F32) for p in P3]
+    scratch += [V((B, C, T, COLS[p]), F32) for p in P3]
+    scratch += [V((B * R * R, C * R, T), F32) for p in P3]
+    scratch += [V((B * R, C * R * R, T), F32) for _ in range(2) for p in P3]
     DMA = pltpu.SemaphoreType.DMA
-    scratch += [DMA((NSEM,)), DMA((NSEM,)), DMA((2, 3)), DMA((2, 3)), DMA((21,)), DMA((6, 4))]
+    scratch += [DMA((NSEM[0],)), DMA((NSEM[1],)), DMA((C, 3)), DMA((C, 3)), DMA((15,)), DMA((3 * C, R))]
     any_spec = pl.BlockSpec(memory_space=pl.ANY)
     vm = pl.BlockSpec(memory_space=pltpu.VMEM)
     out = pl.pallas_call(
@@ -618,7 +602,7 @@
 
 
 def attn_kernel(nb, heads, groups, x_ref, ga_ref, gm_ref, wq_ref, wk_ref, wv_ref, wo_ref, h_ref, z_ref,
-                u_ref, q_ref, k_ref, v_ref, acc_ref):
+                u_ref, acc_ref):
     i = pl.program_id(0)
     seq = x_ref.shape[1]
     d = x_ref.shape[2]
@@ -630,32 +614,23 @@
     def _():
         u_ref[...] = norm(x_ref[...].reshape(nb * seq, d).astype(F32), ga_ref[...])
         acc_ref[...] = jnp.zeros_like(acc_ref)
-        q_ref[...] = jnp.zeros_like(q_ref)
-        k_ref[...] = jnp.zeros_like(k_ref)
-        v_ref[...] = jnp.zeros_like(v_ref)
-
-    q, k, v = q_ref[...], k_ref[...], v_ref[...]
+
     causal = (lax.broadcasted_iota(jnp.int32, (seq, seq), 0) >= lax.broadcasted_iota(jnp.int32, (seq, seq), 1))
     u = u_ref[...]
-    qn = jnp.dot(u, wq_ref[...], preferred_element_type=F32).astype(BF)
-    kn = jnp.dot(u, wk_ref[...], preferred_element_type=F32).astype(BF)
-    vn = jnp.dot(u, wv_ref[...], preferred_element_type=F32).astype(BF)
-    rows = []
-    for b in range(nb):
-        cols = []
-        for hd in range(heads):
-            r, e = slice(b * seq, (b + 1) * seq), slice(hd * HEAD, (hd + 1) * HEAD)
-            s = lax.dot_general(q[r, e], k[r, e], (((1,), (1,)), ((), ())), preferred_element_type=F32) * HEAD ** -0.5
-            s = jnp.where(causal, s, -1e30)
-            p = jnp.exp(s - jnp.max(s, axis=-1, keepdims=True))
-            p = (p / jnp.sum(p, axis=-1, keepdims=True)).astype(BF)
-            cols.append(jnp.dot(p, v[r, e], preferred_element_type=F32).astype(BF))
-        rows.append(jnp.concatenate(cols, axis=1))
-    o = jnp.concatenate(rows, axis=0)
+    q = jnp.dot(u, wq_ref[...], preferred_element_type=F32).astype(BF)
+    k = jnp.dot(u, wk_ref[...], preferred_element_type=F32).astype(BF)
+    v = jnp.dot(u, wv_ref[...], preferred_element_type=F32).astype(BF)
+    units = [(slice(b * seq, (b + 1) * seq), slice(hd * HEAD, (hd + 1) * HEAD)) for b in range(nb) for hd in range(heads)]
+    s = jnp.concatenate([lax.dot_general(q[r, e], k[r, e], (((1,), (1,)), ((), ())), preferred_element_type=F32)[None]
+                         for r, e in units], axis=0)
+    s = jnp.where(causal[None], s * HEAD ** -0.5, -1e30)
+    p = jnp.exp(s - jnp.max(s, axis=-1, keepdims=True))
+    p = (p * (1.0 / jnp.sum(p, axis=-1, keepdims=True))).astype(BF)
+    ov = [jnp.dot(p[j], v[r, e], preferred_element_type=F32).astype(BF) for j, (r, e) in enumerate(units)]
+    o = jnp.concatenate([jnp.concatenate(ov[b * heads:(b + 1) * heads], axis=1) for b in range(nb)], axis=0)
     acc_ref[...] += jnp.dot(o, wo_ref[...], preferred_element_type=F32)
-    q_ref[...], k_ref[...], v_ref[...] = qn, kn, vn
-
-    @pl.when(i == groups)
+
+    @pl.when(i == groups - 1)
     def _():
         h = (x_ref[...].reshape(nb * seq, d).astype(F32) + acc_ref[...]).astype(BF)
         h_ref[...] = h.reshape(nb, seq, d)
@@ -668,19 +643,18 @@
     heads = HEADS_PER_STEP
     cols = heads * HEAD
     groups = width // cols
-    now = lambda i: jnp.minimum(i, groups - 1)
     whole = pl.BlockSpec((nb, seq, d), lambda i: (0, 0, 0))
     gain = pl.BlockSpec((1, d), lambda i: (0, 0))
-    proj = pl.BlockSpec((d, cols), lambda i: (0, now(i)))
+    proj = pl.BlockSpec((d, cols), lambda i: (0, i))
     V = pltpu.VMEM
     return pl.pallas_call(
         functools.partial(attn_kernel, nb, heads, groups),
-        grid=(groups + 1,),
+        grid=(groups,),
         out_shape=[jax.ShapeDtypeStruct((nb, seq, d), BF)] * 2,
         in_specs=[whole, gain, gain, proj, proj, proj,
-                  pl.BlockSpec((cols, d), lambda i: (jnp.maximum(i - 1, 0), 0))],
+                  pl.BlockSpec((cols, d), lambda i: (i, 0))],
         out_specs=[whole, whole],
-        scratch_shapes=[V((nb * seq, d), BF)] + [V((nb * seq, cols), BF)] * 3 + [V((nb * seq, d), F32)],
+        scratch_shapes=[V((nb * seq, d), BF), V((nb * seq, d), F32)],
         compiler_params=pltpu.CompilerParams(dimension_semantics=("arbitrary",), vmem_limit_bytes=VMEM_LIMIT),
     )(x, gattn.reshape(1, d), gmoe.reshape(1, d), wq, wk, wv, wo)
 

time: 338 us -> 318 us (0.941)
  Pallas kernels: 335 us -> 315 us
    pallas_call x1, Pallas kernels: 49 us -> 32.3 us  [attention(): pl.pallas_call(functools.partial(attn_kernel, nb, heads, groups), grid=(g...]
    pallas_call x1, Pallas kernels: 287 us -> 283 us  [moe(): pl.pallas_call(functools.partial(moe_kernel, dims, NSEM), out_shape=[jax....]
where the time goes in v3:
time: 318 us; the launch traced here: 317 us
  Pallas kernels  315 us (99%)
    pallas_call x1, Pallas kernels, moe(): pl.pallas_call(functools.partial(moe_kernel, dims, NSEM), out_shape=[jax....  283 us
    pallas_call x1, Pallas kernels, attention(): pl.pallas_call(functools.partial(attn_kernel, nb, heads, groups), grid=(g...  32.3 us

profile of v3, /device:TPU:0, one launch (start us, length us, event | category | flops | bytes accessed | tf_op | source)
XLA Modules:
  0.0 317.3 jit_solution(4085199964518235602)
XLA Ops:
  0.0 32.3 %shard_map.118 = (bf16[2,128,2048]{2,1,0:T(8,128)(2,1)}, bf16[2,128,2048]{2,1,0:T(8,128)(2,1)}) custom-call(bf16[2,128,2048]{2,1,0:T(8,128)(2,1)} %bitcast.12, f32[1,2048]{1,0:T(1,128)} %bitcast.14, f32[1,2048]{1,0:T(1,128)} %bitcast.15, bf16[2048,4096]{1,0:T(8,128)(2,1)} %wq_ref.1, bf16[2048,4096]{1,0:T(8,128)(2,1)} %wk_ref.1, bf16[2048,4096]{1,0:T(8,128)(2,1)} %wv_ref.1, ...), custom_call_target="tpu_custom_call" | custom-call | tf_op jit(solution)/shard_map/pallas_call | solution.py:650
  32.3 282.7 %shard_map.119 = (bf16[2,128,2048]{2,1,0:T(8,128)(2,1)}, bf16[2,2,4,4,4,16,640]{6,5,4,3,2,1,0:T(8,128)(2,1)}, bf16[2,2,4,4,4,16,640]{6,5,4,3,2,1,0:T(8,128)(2,1)...) custom-call(bf16[2,128,2048]{2,1,0:T(8,128)(2,1)} %get-tuple-element, ...), custom_call_target="tpu_custom_call" | custom-call | tf_op jit(solution)/shard_map/pallas_call | solution.py:593
  315.0 2.3 copy.15

commit v4 on v3

--- a/solution.py
+++ b/solution.py
@@ -9,7 +9,7 @@
 
 HEAD = 128
 VMEM_LIMIT = 67_000_000
-HEADS_PER_STEP = 4
+HEADS_PER_STEP = 8
 ORDER = (
     "mt1", "a1_00", "a1_01", "a1_10", "a1_11", "a1_02", "mt2", "a2_02", "a2_00", "a2_01", "a1_12", "mt3", "a3_02",
     "a3_00", "a3_01", "a2_10", "mt4", "a2_11", "a2_12", "a4_00", "a4_02", "a3_11", "a3_12", "a4_01", "a3_10", "tab",
@@ -49,8 +49,8 @@
         return self.n - k
 
 
-def moe_kernel(dims, nsem, z_hbm, h_ref, idx_ref, gate_ref, w1_hbm, w3_hbm, w2_hbm,
-               y_ref, *rest):
+def moe_kernel(dims, nsem, z_hbm, h_hbm, idx_ref, gate_ref, w1_hbm, w3_hbm, w2_hbm,
+               y_hbm, *rest):
     T, D, FF, CAP, TOP, COLS = dims
     it = iter(rest)
     recv = [next(it) for _ in range(3)]
@@ -69,6 +69,7 @@
     part_acc = [next(it) for _ in range(3)]
     q1 = [next(it) for _ in range(3)]
     q2 = [next(it) for _ in range(3)]
+    h_ref, y_ref = next(it), next(it)
     drank = [next(it) for _ in range(3)]
     crank = [next(it) for _ in range(3)]
     cgate = [next(it) for _ in range(3)]
@@ -108,11 +109,6 @@
     friends.append({"row": 1 - c, "col": q})
     for f in friends:
         pl.semaphore_signal(barrier, inc=1, device_id=f, device_id_type=MESH)
-    wload = []
-    for i, (a, b) in enumerate(((w1_hbm, w1), (w3_hbm, w3), (w2_hbm, w2))):
-        cp = pltpu.make_async_copy(a.at[0], b, lsem.at[i])
-        cp.start()
-        wload.append(cp)
     own = {}
     for m in range(2):
         for p, (d1, d2, d3) in enumerate(PARTS):
@@ -120,6 +116,13 @@
                                        lsem.at[3 + m * 3 + p])
             cp.start()
             own[m, p] = cp
+    wload = []
+    for i, (a, b) in enumerate(((w1_hbm, w1), (w3_hbm, w3), (w2_hbm, w2))):
+        cp = pltpu.make_async_copy(a.at[0], b, lsem.at[i])
+        cp.start()
+        wload.append(cp)
+    hload = pltpu.make_async_copy(h_hbm, h_ref, lsem.at[15])
+    hload.start()
     for p, (d1, d2, d3) in enumerate(PARTS):
         mi[p, pos[d2], pos[d1]] = idx_ref[...]
         mg[p, pos[d1]] = gate_ref[...]
@@ -478,12 +481,17 @@
         part_acc[p][m, 3, half:T] = part_acc[p][m, 3, half:T] + q1[p][m, 1]
         send(part_acc[p].at[m, 3], q2[p].at[m, 1], nb(dim, -1), st["s"], st["r"])
 
+    def y_store(m, p):
+        cols = pl.ds(offs[p], COLS[p])
+        return pltpu.make_async_copy(y_ref.at[m, :, cols], y_hbm.at[m, :, cols], lsem.at[3 + m * 3 + p])
+
     def r3_end(m, p):
         wait_in(q2[p].at[m], r3[m, p]["r"])
         unsent.append((part_acc[p].at[m, pl.ds(0, 3)], r3[m, p]["s"]))
         cols = slice(offs[p], offs[p] + COLS[p])
         acc = part_acc[p][m, 0] + q2[p][m, 0] + q2[p][m, 1]
         y_ref[m, :, cols] = (h_ref[m, :, cols].astype(F32) + acc).astype(BF)
+        y_store(m, p).start()
 
     meta = {}
 
@@ -550,12 +558,15 @@
             else:
                 events.setdefault(at, []).append(functools.partial(do, nxt))
         if m == 0:
-            for cp in wload:
+            for cp in wload + [hload]:
                 cp.wait()
         p_wait(m)
         expert(m, events)
     for ref, si in unsent:
         wait_out(ref, si)
+    for m in range(2):
+        for p in P3:
+            y_store(m, p).wait()
     if (S.n, R.n) != nsem:
         raise ValueError(f"{S.n} {R.n}")
 
@@ -584,57 +595,75 @@
     scratch += [V((B, R, T, COLS[p]), F32) for p in P3]
     scratch += [V((B, C, T // 2, COLS[p]), F32) for p in P3]
     scratch += [V((B, C, T, COLS[p]), F32) for p in P3]
+    scratch += [V((B, T, D), BF)] * 2
     scratch += [V((B * R * R, C * R, T), F32) for p in P3]
     scratch += [V((B * R, C * R * R, T), F32) for _ in range(2) for p in P3]
     DMA = pltpu.SemaphoreType.DMA
-    scratch += [DMA((NSEM[0],)), DMA((NSEM[1],)), DMA((C, 3)), DMA((C, 3)), DMA((15,)), DMA((3 * C, R))]
+    scratch += [DMA((NSEM[0],)), DMA((NSEM[1],)), DMA((C, 3)), DMA((C, 3)), DMA((16,)), DMA((3 * C, R))]
     any_spec = pl.BlockSpec(memory_space=pl.ANY)
     vm = pl.BlockSpec(memory_space=pltpu.VMEM)
     out = pl.pallas_call(
         functools.partial(moe_kernel, dims, NSEM),
         out_shape=[jax.ShapeDtypeStruct((2, T, D), BF)] + hbm,
-        in_specs=[any_spec, vm, vm, vm, any_spec, any_spec, any_spec],
-        out_specs=[vm] + [any_spec] * len(hbm),
+        in_specs=[any_spec, any_spec, vm, vm, any_spec, any_spec, any_spec],
+        out_specs=[any_spec] * (1 + len(hbm)),
         scratch_shapes=scratch,
         compiler_params=pltpu.CompilerParams(collective_id=0, has_side_effects=True, vmem_limit_bytes=VMEM_LIMIT),
     )(z, h, idx, gates, w1, w3, w2)
     return out[0]
 
 
-def attn_kernel(nb, heads, groups, x_ref, ga_ref, gm_ref, wq_ref, wk_ref, wv_ref, wo_ref, h_ref, z_ref,
-                u_ref, acc_ref):
-    i = pl.program_id(0)
-    seq = x_ref.shape[1]
-    d = x_ref.shape[2]
+def attn_kernel(nb, heads, groups, x_ref, ga_ref, gm_ref, wq_hbm, wk_hbm, wv_hbm, wo_hbm, h_ref, z_ref,
+                wq, wk, wv, wo, u_ref, acc_ref, sem):
+    seq, d = x_ref.shape[1:]
+    cols = heads * HEAD
 
     def norm(v, g):
         return (v * lax.rsqrt(jnp.mean(v * v, axis=-1, keepdims=True) + 1e-6) * g).astype(BF)
 
-    @pl.when(i == 0)
-    def _():
-        u_ref[...] = norm(x_ref[...].reshape(nb * seq, d).astype(F32), ga_ref[...])
-        acc_ref[...] = jnp.zeros_like(acc_ref)
-
+    def loads(i, slot):
+        part = pl.ds(pl.multiple_of(i * cols, HEAD), cols)
+        pairs = ((wq_hbm.at[:, part], wq), (wk_hbm.at[:, part], wk), (wv_hbm.at[:, part], wv), (wo_hbm.at[part], wo))
+        return [pltpu.make_async_copy(src, dst.at[slot], sem.at[slot, j]) for j, (src, dst) in enumerate(pairs)]
+
+    for cp in loads(0, 0):
+        cp.start()
+    u_ref[...] = norm(x_ref[...].reshape(nb * seq, d).astype(F32), ga_ref[...])
+    acc_ref[...] = jnp.zeros_like(acc_ref)
     causal = (lax.broadcasted_iota(jnp.int32, (seq, seq), 0) >= lax.broadcasted_iota(jnp.int32, (seq, seq), 1))
-    u = u_ref[...]
-    q = jnp.dot(u, wq_ref[...], preferred_element_type=F32).astype(BF)
-    k = jnp.dot(u, wk_ref[...], preferred_element_type=F32).astype(BF)
-    v = jnp.dot(u, wv_ref[...], preferred_element_type=F32).astype(BF)
     units = [(slice(b * seq, (b + 1) * seq), slice(hd * HEAD, (hd + 1) * HEAD)) for b in range(nb) for hd in range(heads)]
-    s = jnp.concatenate([lax.dot_general(q[r, e], k[r, e], (((1,), (1,)), ((), ())), preferred_element_type=F32)[None]
-                         for r, e in units], axis=0)
-    s = jnp.where(causal[None], s * HEAD ** -0.5, -1e30)
-    p = jnp.exp(s - jnp.max(s, axis=-1, keepdims=True))
-    p = (p * (1.0 / jnp.sum(p, axis=-1, keepdims=True))).astype(BF)
-    ov = [jnp.dot(p[j], v[r, e], preferred_element_type=F32).astype(BF) for j, (r, e) in enumerate(units)]
-    o = jnp.concatenate([jnp.concatenate(ov[b * heads:(b + 1) * heads], axis=1) for b in range(nb)], axis=0)
-    acc_ref[...] += jnp.dot(o, wo_ref[...], preferred_element_type=F32)
-
-    @pl.when(i == groups - 1)
-    def _():
-        h = (x_ref[...].reshape(nb * seq, d).astype(F32) + acc_ref[...]).astype(BF)
-        h_ref[...] = h.reshape(nb, seq, d)
-        z_ref[...] = norm(h.astype(F32), gm_ref[...]).reshape(nb, seq, d)
+
+    def group(i, _):
+        slot = i % 2
+
+        @pl.when(i + 1 < groups)
+        def _():
+            for cp in loads(i + 1, (i + 1) % 2):
+                cp.start()
+
+        here = loads(i, slot)
+
+        def proj(j, w):
+            here[j].wait()
+            return jnp.dot(u_ref[...], w[slot], preferred_element_type=F32).astype(BF)
+
+        q, k = proj(0, wq), proj(1, wk)
+        s = jnp.concatenate([lax.dot_general(q[r, e], k[r, e], (((1,), (1,)), ((), ())), preferred_element_type=F32)[None]
+                             for r, e in units], axis=0)
+        s = jnp.where(causal[None], s * HEAD ** -0.5, -1e30)
+        p = jnp.exp(s - jnp.max(s, axis=-1, keepdims=True))
+        p = (p * (1.0 / jnp.sum(p, axis=-1, keepdims=True))).astype(BF)
+        v = proj(2, wv)
+        ov = [jnp.dot(p[j], v[r, e], preferred_element_type=F32).astype(BF) for j, (r, e) in enumerate(units)]
+        o = jnp.concatenate([jnp.concatenate(ov[b * heads:(b + 1) * heads], axis=1) for b in range(nb)], axis=0)
+        here[3].wait()
+        acc_ref[...] += jnp.dot(o, wo[slot], preferred_element_type=F32)
+        return 0
+
+    lax.fori_loop(0, groups, group, 0)
+    h = (x_ref[...].reshape(nb * seq, d).astype(F32) + acc_ref[...]).astype(BF)
+    h_ref[...] = h.reshape(nb, seq, d)
+    z_ref[...] = norm(h.astype(F32), gm_ref[...]).reshape(nb, seq, d)
 
 
 def attention(x, wq, wk, wv, wo, gattn, gmoe):
@@ -642,20 +671,16 @@
     width = wq.shape[1]
     heads = HEADS_PER_STEP
     cols = heads * HEAD
-    groups = width // cols
-    whole = pl.BlockSpec((nb, seq, d), lambda i: (0, 0, 0))
-    gain = pl.BlockSpec((1, d), lambda i: (0, 0))
-    proj = pl.BlockSpec((d, cols), lambda i: (0, i))
     V = pltpu.VMEM
+    vm, any_spec = pl.BlockSpec(memory_space=V), pl.BlockSpec(memory_space=pl.ANY)
     return pl.pallas_call(
-        functools.partial(attn_kernel, nb, heads, groups),
-        grid=(groups,),
+        functools.partial(attn_kernel, nb, heads, width // cols),
         out_shape=[jax.ShapeDtypeStruct((nb, seq, d), BF)] * 2,
-        in_specs=[whole, gain, gain, proj, proj, proj,
-                  pl.BlockSpec((cols, d), lambda i: (i, 0))],
-        out_specs=[whole, whole],
-        scratch_shapes=[V((nb * seq, d), BF), V((nb * seq, d), F32)],
-        compiler_params=pltpu.CompilerParams(dimension_semantics=("arbitrary",), vmem_limit_bytes=VMEM_LIMIT),
+        in_specs=[vm] * 3 + [any_spec] * 4,
+        out_specs=[vm, vm],
+        scratch_shapes=[V((2, d, cols), BF)] * 3 + [V((2, cols, d), BF), V((nb * seq, d), BF), V((nb * seq, d), F32),
+                                                    pltpu.SemaphoreType.DMA((2, 4))],
+        compiler_params=pltpu.CompilerParams(vmem_limit_bytes=VMEM_LIMIT),
     )(x, gattn.reshape(1, d), gmoe.reshape(1, d), wq, wk, wv, wo)
 
 

time: 318 us -> 314 us (0.987)
  Pallas kernels: 315 us -> 310 us
    pallas_call x1, Pallas kernels: 32.3 us -> 29 us  [attention(): pl.pallas_call(functools.partial(attn_kernel, nb, heads, width // cols),...]
where the time goes in v4:
time: 314 us; the launch traced here: 312 us
  Pallas kernels  310 us (99%)
    pallas_call x1, Pallas kernels, moe(): pl.pallas_call(functools.partial(moe_kernel, dims, NSEM), out_shape=[jax....  281 us
    pallas_call x1, Pallas kernels, attention(): pl.pallas_call(functools.partial(attn_kernel, nb, heads, width // cols),...  29 us

profile of v4, /device:TPU:0, one launch (start us, length us, event | category | flops | bytes accessed | tf_op | source)
XLA Modules:
  0.0 312.4 jit_solution(13209096098902179262)
XLA Ops:
  0.0 29.0 %shard_map.118 = (bf16[2,128,2048]{2,1,0:T(8,128)(2,1)}, bf16[2,128,2048]{2,1,0:T(8,128)(2,1)}) custom-call(bf16[2,128,2048]{2,1,0:T(8,128)(2,1)} %bitcast.12, f32[1,2048]{1,0:T(1,128)} %bitcast.14, f32[1,2048]{1,0:T(1,128)} %bitcast.15, bf16[2048,4096]{1,0:T(8,128)(2,1)} %wq_hbm.1, bf16[2048,4096]{1,0:T(8,128)(2,1)} %wk_hbm.1, bf16[2048,4096]{1,0:T(8,128)(2,1)} %wv_hbm.1, ...), custom_call_target="tpu_custom_call" | custom-call | tf_op jit(solution)/shard_map/pallas_call | solution.py:676
  29.0 281.1 %shard_map.119 = (bf16[2,128,2048]{2,1,0:T(8,128)(2,1)}, bf16[2,2,4,4,4,16,640]{6,5,4,3,2,1,0:T(8,128)(2,1)}, bf16[2,2,4,4,4,16,640]{6,5,4,3,2,1,0:T(8,128)(2,1)...) custom-call(bf16[2,128,2048]{2,1,0:T(8,128)(2,1)} %get-tuple-element, ...), custom_call_target="tpu_custom_call" | custom-call | tf_op jit(solution)/shard_map/pallas_call | solution.py:605
  310.1 2.3 copy.15

commit v5 on v4

--- a/solution.py
+++ b/solution.py
@@ -610,7 +610,33 @@
         scratch_shapes=scratch,
         compiler_params=pltpu.CompilerParams(collective_id=0, has_side_effects=True, vmem_limit_bytes=VMEM_LIMIT),
     )(z, h, idx, gates, w1, w3, w2)
-    return out[0]
+    return settle(out[0])
+
+
+def settle_kernel(chunks, src, dst, buf, isem, osem):
+    rows = src.shape[1] // chunks
+    parts = [(m, pl.ds(i * rows, rows)) for m in range(src.shape[0]) for i in range(chunks)]
+    ins = [pltpu.make_async_copy(src.at[p], buf.at[p], isem.at[j]) for j, p in enumerate(parts)]
+    outs = [pltpu.make_async_copy(buf.at[p], dst.at[p], osem.at[j]) for j, p in enumerate(parts)]
+    for cp in ins:
+        cp.start()
+    for a, b in zip(ins, outs):
+        a.wait()
+        b.start()
+    for cp in outs:
+        cp.wait()
+
+
+def settle(y):
+    chunks = 2
+    n = y.shape[0] * chunks
+    any_spec = pl.BlockSpec(memory_space=pl.ANY)
+    return pl.pallas_call(
+        functools.partial(settle_kernel, chunks), out_shape=jax.ShapeDtypeStruct(y.shape, y.dtype),
+        in_specs=[any_spec], out_specs=any_spec,
+        scratch_shapes=[pltpu.VMEM(y.shape, y.dtype), pltpu.SemaphoreType.DMA((n,)), pltpu.SemaphoreType.DMA((n,))],
+        compiler_params=pltpu.CompilerParams(vmem_limit_bytes=VMEM_LIMIT),
+    )(y)
 
 
 def attn_kernel(nb, heads, groups, x_ref, ga_ref, gm_ref, wq_hbm, wk_hbm, wv_hbm, wo_hbm, h_ref, z_ref,

time: 314 us -> 314 us (level)
  no operation moved by 1% of the time
where the time goes in v5:
time: 314 us; the launch traced here: 312 us
  Pallas kernels  312 us (99%)
    pallas_call x1, Pallas kernels, moe(): pl.pallas_call(functools.partial(moe_kernel, dims, NSEM), out_shape=[jax....  281 us
    pallas_call x1, Pallas kernels, attention(): pl.pallas_call(functools.partial(attn_kernel, nb, heads, width // cols),...  29 us

profile of v5, /device:TPU:0, one launch (start us, length us, event | category | flops | bytes accessed | tf_op | source)
XLA Modules:
  0.0 312.3 jit_solution(9575147199113295156)
XLA Ops:
  0.0 29.0 %shard_map.118 = (bf16[2,128,2048]{2,1,0:T(8,128)(2,1)}, bf16[2,128,2048]{2,1,0:T(8,128)(2,1)}) custom-call(bf16[2,128,2048]{2,1,0:T(8,128)(2,1)} %bitcast.12, f32[1,2048]{1,0:T(1,128)} %bitcast.13, f32[1,2048]{1,0:T(1,128)} %bitcast.14, bf16[2048,4096]{1,0:T(8,128)(2,1)} %wq_hbm.1, bf16[2048,4096]{1,0:T(8,128)(2,1)} %wk_hbm.1, bf16[2048,4096]{1,0:T(8,128)(2,1)} %wv_hbm.1, ...), custom_call_target="tpu_custom_call" | custom-call | tf_op jit(solution)/shard_map/pallas_call | solution.py:702
  29.0 281.1 %shard_map.119 = (bf16[2,128,2048]{2,1,0:T(8,128)(2,1)}, bf16[2,2,4,4,4,16,640]{6,5,4,3,2,1,0:T(8,128)(2,1)}, bf16[2,2,4,4,4,16,640]{6,5,4,3,2,1,0:T(8,128)(2,1)...) custom-call(bf16[2,128,2048]{2,1,0:T(8,128)(2,1)} %get-tuple-element, ...), custom_call_target="tpu_custom_call" | custom-call | tf_op jit(solution)/shard_map/pallas_call | solution.py:605
  310.1 2.0 shard_map.120
